TPU v7x, 128 devices: a whole 4x4x4 slice. The times are simulated.
128 devices in a mesh: row: 8 (over z, core), col: 16 (over y, x).
Axes of the slice: x: 4, y: 4, z: 4, core: 2. Of those that a mesh axis runs over, the one named last changes fastest.
Arguments:
- src_field: bfloat16 [64, 4194304], P(None, ('row', 'col')), may hold values from 0.5 to 2
- src_area: float32 [4194304], P(('row', 'col')), may hold values from 0.3 to 3
- tgt_area: float32 [1048576], P(('row', 'col')), may hold values from 0.3 to 3
- weights: bfloat16 [49152, 128, 128], P(('row', 'col')), may hold values from 0 to 0.0025939941
- send_index: int32 [128, 128, 2], P(('row', 'col')), may hold values from -1 to 255, as said below
- pair_slot: int32 [49152], P(('row', 'col')), may hold values from 0 to 255, as said below
- pair_target: int32 [49152], P(('row', 'col')), may hold values from 0 to 63, as said below
Outputs:
- target_field: float32 [64, 1048576], P(None, ('row', 'col'))
Inputs may be any that keep to these rules, and one draw needn't show every extreme that they name: `send_index`: in each [s, r] the live entries (not -1) come first and there are 1 to 2 of them; every sender sends to every receiver; for each receiver some sender fills all 2 slots. `pair_slot`: each pair of device r names a live slot of what device r receives; every live slot is named by some pair of device r. `pair_target`: every local target block of a device is named by some pair of that device.
All inputs are finite; a program needn't handle non-finite values.
Results may differ from a plain program's by a relative error of at most 0.0003.
Values may be sent and summed in bfloat16 or wider, within the bound.
A program may use at most 128 MiB of HBM per device.

v0:
```python
import jax
import jax.numpy as jnp
from jax import lax
from jax.sharding import Mesh
from jax.sharding import PartitionSpec as P

ROW_COL = ("row_0", "row_1", "col_0", "col_1")


def by_axis(value, axes):
    for axis in axes:
        value = lax.psum(value, axis)
    return value


def shards(src_field, src_area, tgt_area, weights, send_index, pair_slot, pair_target):
    columns, cell_count = src_field.shape
    block_size = weights.shape[1]
    local_blocks = cell_count // block_size
    target_blocks = tgt_area.shape[0] // block_size
    send_rows = send_index[0]
    peer_count, capacity = send_rows.shape
    blocks = src_field.reshape(columns, local_blocks, block_size)
    source_local = jnp.sum(src_field.astype(jnp.float32) * src_area[None, :], axis=1)
    chosen = jnp.maximum(send_rows.reshape(-1), 0)
    outbound = jnp.take(blocks, chosen, axis=1)
    outbound = jnp.transpose(outbound, (1, 0, 2)).reshape(peer_count, capacity, columns, block_size)
    inbound = lax.all_to_all(outbound, ROW_COL, split_axis=0, concat_axis=0, tiled=True)
    inbound = inbound.reshape(peer_count * capacity, columns, block_size)
    picked = jnp.take(inbound, pair_slot, axis=0)
    products = jnp.einsum("pcs,pst->pct", picked, weights, preferred_element_type=jnp.float32)
    placed = jax.ops.segment_sum(products, pair_target, num_segments=target_blocks)
    regridded = jnp.transpose(placed, (1, 0, 2)).reshape(columns, target_blocks * block_size)
    target_local = jnp.sum(regridded * tgt_area[None, :], axis=1)
    source_mass, target_mass = (by_axis(source_local, ROW_COL), by_axis(target_local, ROW_COL))
    return regridded * (source_mass / target_mass)[:, None]


def solution(mesh):
    split = Mesh(mesh.devices.reshape(4, 2, 4, 4), ("row_0", "row_1", "col_0", "col_1"))
    placed = (
        P(None, ROW_COL),
        P(ROW_COL),
        P(ROW_COL),
        P(ROW_COL, None, None),
        P(ROW_COL, None, None),
        P(ROW_COL),
        P(ROW_COL),
    )
    return jax.shard_map(
        shards, mesh=split, in_specs=placed, out_specs=P(None, ROW_COL), check_vma=False
    )
```

profile of v0, /device:TPU:0, one launch (start us, length us, event | category | flops | bytes accessed | tf_op | source)
XLA Modules:
  0.0 171.6 jit_solution(789475034657432095)
XLA Ops:
  0.0 0.7 broadcast_maximum_fusion
  0.7 0.7 broadcast_compare_fusion
  1.4 5.3 %copy_bitcast_fusion = bf16[64,256,128]{2,0,1:T(8,128)(2,1)} fusion(bf16[64,32768]{1,0:T(8,128)(2,1)} %param.7), kind=kLoop, calls=%fused_computation.7 | loop fusion | bytes 8388608 | tf_op jit(solution)/shard_map/reshape | solution.py:23
  6.7 0.1 copy.11
  6.8 0.1 reshape.53
  7.0 0.1 copy.10
  7.1 0.1 le.27
  7.2 5.3 %gather_fusion = bf16[256,64,128]{2,1,0:T(8,128)(2,1)} fusion(bf16[64,256,128]{2,0,1:T(8,128)(2,1)} %copy_bitcast_fusion, s32[1024]{0:T(1024)S(1)} %pad_clamp_fusion.1), kind=kCustom, calls=%fused_computation | custom fusion | bytes 8389632 | tf_op jit(solution)/shard_map/jit(_take)/gather | solution.py:26
  12.5 4.0 %broadcast_select_fusion = bf16[256,64,128]{2,1,0:T(8,128)(2,1)} fusion(bf16[256,64,128]{2,1,0:T(8,128)(2,1)} %gather_fusion, pred[256]{0:T(512)(128)(4,1)S(1)} %le.27), kind=kLoop, calls=%fused_computation.8 | loop fusion | flops 2097152 | bytes 8388864 | tf_op jit(solution)/shard_map/jit(_take)/select_n | solution.py:26
  16.5 0.0 copy-start.2
  16.5 0.0 copy-start
  16.5 11.7 %all-to-all-start = ((bf16[128,2,64,128]{3,2,1,0:T(8,128)(2,1)}), bf16[128,2,64,128]{3,2,1,0:T(8,128)(2,1)}, u32[]{:S(2)}, u32[]{:S(2)}) async-start(bf16[128,2,64,128]{3,2,1,0:T(8,128)(2,1)} %bitcast.18), calls=%async_computation | async-start | bytes 8388608 | tf_op jit(solution)/shard_map/all_to_all | solution.py:28
  28.2 0.0 copy-done.2
  28.3 0.0 copy-done
  28.3 3.1 %multiply_reduce_fusion = f32[64]{0:T(128)S(1)} fusion(bf16[64,32768]{1,0:T(8,128)(2,1)} %param.7, f32[32768]{0:T(1024)S(1)} %copy-done), kind=kLoop, calls=%fused_computation.3 | loop fusion | flops 6291392 | bytes 4325632 | tf_op jit(solution)/shard_map/reduce_sum | solution.py:24
  31.4 47.5 %all-to-all-done = bf16[128,2,64,128]{3,2,1,0:T(8,128)(2,1)} async-done(((bf16[128,2,64,128]{3,2,1,0:T(8,128)(2,1)}), bf16[128,2,64,128]{3,2,1,0:T(8,128)(2,1)}, u32[]{:S(2)}, u32[]{:S(2)}) %all-to-all-start) | async-done | bytes 4194336 | tf_op jit(solution)/shard_map/all_to_all | solution.py:28
  78.9 6.2 %gather_fusion.1 = bf16[384,64,128]{2,1,0:T(8,128)(2,1)} fusion(bf16[256,64,128]{2,1,0:T(8,128)(2,1)} %bitcast.1, s32[1024]{0:T(1024)S(1)} %pad_clamp_fusion), kind=kCustom, calls=%fused_computation.1 | custom fusion | bytes 12584448 | tf_op jit(solution)/shard_map/jit(_take)/gather | solution.py:30
  85.0 0.0 copy-start.3
  85.0 14.4 %fusion = f32[384,64,128]{2,1,0:T(8,128)} fusion(bf16[384,128,128]{2,1,0:T(8,128)(2,1)} %param.10, bf16[384,64,128]{2,1,0:T(8,128)(2,1)} %gather_fusion.1, pred[384]{0:T(512)(128)(4,1)S(1)} %compare_and_fusion), kind=kOutput, calls=%fused_computation.4 | convolution fusion | flops 808452096 | bytes 31457664 | tf_op jit(solution)/shard_map/pcs,pst->pct/dot_general | solution.py:31
  99.5 0.2 broadcast_in_dim.31
  99.7 0.0 copy-done.3
  99.7 0.0 copy-start.1
  99.7 39.5 %scatter_fusion = f32[64,64,128]{2,1,0:T(8,128)S(1)} fusion(f32[64,64,128]{2,1,0:T(8,128)S(1)} %broadcast_in_dim.31, s32[384]{0:T(512)S(1)} %copy-done.3, f32[384,64,128]{2,1,0:T(8,128)} %fusion), kind=kCustom, calls=%fused_computation.2 | custom fusion | flops 3145728 | bytes 37750272 | tf_op jit(solution)/shard_map/scatter-add | solution.py:32
  139.3 0.0 copy-done.1
  139.3 0.3 fusion.4
  139.6 9.9 %all-reduce.2 = (f32[64]{0:T(128)S(1)}, f32[64]{0:T(128)S(1)}) all-reduce(f32[64]{0:T(128)S(1)} %multiply_reduce_fusion, f32[64]{0:T(128)S(1)} %fusion.4), channel_id=1, replica_groups=mesh['row_0'=4,'row_1'=2,'col_0'=4,'col_1'=4] {'row_0'}, use_global_device_ids=true, to_apply=%region_2.3 | all-reduce | flops 128 | bytes 1024 | tf_op jit(solution)/shard_map/psum | solution.py:12
  149.5 2.5 %all-reduce.3 = (f32[64]{0:T(128)S(1)}, f32[64]{0:T(128)S(1)}) all-reduce(f32[64]{0:T(128)S(1)} %get-tuple-element.9, f32[64]{0:T(128)S(1)} %get-tuple-element.10), channel_id=1, replica_groups=mesh['row_0'=4,'row_1'=2,'col_0'=4,'col_1'=4] {'row_1'}, use_global_device_ids=true, to_apply=%region_3.4 | all-reduce | flops 128 | bytes 1024 | tf_op jit(solution)/shard_map/psum | solution.py:12
  151.9 8.4 %all-reduce.1 = (f32[64]{0:T(128)S(1)}, f32[64]{0:T(128)S(1)}) all-reduce(f32[64]{0:T(128)S(1)} %get-tuple-element.11, f32[64]{0:T(128)S(1)} %get-tuple-element.12), channel_id=1, replica_groups=mesh['row_0'=4,'row_1'=2,'col_0'=4,'col_1'=4] {'col_0'}, use_global_device_ids=true, to_apply=%region_4.5 | all-reduce | flops 128 | bytes 1024 | tf_op jit(solution)/shard_map/psum | solution.py:12
  160.3 9.7 %all-reduce = (f32[64]{0:T(128)S(1)}, f32[64]{0:T(128)S(1)}) all-reduce(f32[64]{0:T(128)S(1)} %get-tuple-element.7, f32[64]{0:T(128)S(1)} %get-tuple-element.8), channel_id=1, replica_groups=mesh['row_0'=4,'row_1'=2,'col_0'=4,'col_1'=4] {'col_1'}, use_global_device_ids=true, to_apply=%region_5.6 | all-reduce | flops 128 | bytes 1024 | tf_op jit(solution)/shard_map/psum | solution.py:12
  170.0 1.5 bitcast_multiply_fusion
  (5 shorter events, 0.0 us)
Async XLA Ops:
  16.5 11.7 %copy-start.2 = (s32[384]{0:T(512)S(1)}, s32[384]{0:T(512)}, u32[]{:S(2)}) copy-start(s32[384]{0:T(512)} %param.12) | copy-start | bytes 4612
  16.5 11.8 %copy-start = (f32[32768]{0:T(1024)S(1)}, f32[32768]{0:T(1024)}, u32[]{:S(2)}) copy-start(f32[32768]{0:T(1024)} %param.8) | copy-start | bytes 393220
  16.5 62.3 %all-to-all-start = ((bf16[128,2,64,128]{3,2,1,0:T(8,128)(2,1)}), bf16[128,2,64,128]{3,2,1,0:T(8,128)(2,1)}, u32[]{:S(2)}, u32[]{:S(2)}) async-start(bf16[128,2,64,128]{3,2,1,0:T(8,128)(2,1)} %bitcast.18), calls=%async_computation | async-start | bytes 8388608 | tf_op jit(solution)/shard_map/all_to_all | solution.py:28
  85.0 14.7 %copy-start.3 = (s32[384]{0:T(512)S(1)}, s32[384]{0:T(512)}, u32[]{:S(2)}) copy-start(s32[384]{0:T(512)} %param.13) | copy-start | bytes 4612
  99.7 39.5 %copy-start.1 = (f32[8192]{0:T(1024)S(1)}, f32[8192]{0:T(1024)}, u32[]{:S(2)}) copy-start(f32[8192]{0:T(1024)} %param.9) | copy-start | bytes 98308
where the time goes:
time: 173 us; the launch traced here: 172 us
  other arithmetic  49.8 us (29%)
  waiting for transfers between devices  47.5 us (27%)
  blocking collectives  30.5 us (18%)
  local copies, waits for them, and re-layouts  17.5 us (10%)
  matrix products  14.4 us (8%)
  starting transfers between devices  11.7 us (7%)
    all_to_all x1, waiting for transfers between devices, shards(): lax.all_to_all(outbound, ROW_COL, split_axis=0, concat_axis=0, tiled=True)  47.5 us
    scatter-add x1, other arithmetic, shards(): jax.ops.segment_sum(products, pair_target, num_segments=target_blocks)  39.5 us
    psum x4, blocking collectives, by_axis(): value = lax.psum(value, axis)  30.5 us
    dot_general x1, matrix products, shards(): jnp.einsum('pcs,pst->pct', picked, weights, preferred_element_type=jnp.fl...  14.4 us
    all_to_all x1, starting transfers between devices, shards(): lax.all_to_all(outbound, ROW_COL, split_axis=0, concat_axis=0, tiled=True)  11.7 us
    gather x1, local copies, waits for them, and re-layouts, shards(): picked = jnp.take(inbound, pair_slot, axis=0)  6.17 us
    reshape x1, local copies, waits for them, and re-layouts, shards(): blocks = src_field.reshape(columns, local_blocks, block_size)  5.32 us
    gather x1, local copies, waits for them, and re-layouts, shards(): outbound = jnp.take(blocks, chosen, axis=1)  5.25 us
  transfers between devices with their start and end apart: 1, of which 1 were waited for; matrix products, arithmetic and copies ran while one was open for 2% of the time, Pallas kernels for 0%

commit v1 on v0

v1 whole, which is shorter than its diff:
```python
import functools

import jax
import jax.numpy as jnp
from jax import lax
from jax.experimental import pallas as pl
from jax.experimental.pallas import tpu as pltpu
from jax.sharding import Mesh
from jax.sharding import PartitionSpec as P

AXES = ("z", "core", "y", "x")
SIZES = (4, 2, 4, 4)
BLOCK = 128
GATHERED = 16
PAIRS = 32


def collect(index_ref, source_ref, out_ref):
    first = pl.program_id(0) * GATHERED
    for i in range(GATHERED):
        block = jnp.maximum(index_ref[0, i % 2, first // 2 + i // 2], 0)
        columns = pl.ds(pl.multiple_of(block * BLOCK, BLOCK), BLOCK)
        out_ref[i] = source_ref[:, columns]


def outbound_blocks(send_index, source):
    rows, cells = source.shape
    peers, capacity = send_index.shape[1:]
    slots = peers * capacity
    return pl.pallas_call(
        collect,
        out_shape=jax.ShapeDtypeStruct((slots, rows, BLOCK), source.dtype),
        grid_spec=pltpu.PrefetchScalarGridSpec(
            num_scalar_prefetch=1,
            grid=(slots // GATHERED,),
            in_specs=[pl.BlockSpec((rows, cells), lambda i, s: (0, 0))],
            out_specs=pl.BlockSpec((GATHERED, rows, BLOCK), lambda i, s: (i, 0, 0)),
        ),
    )(jnp.swapaxes(send_index, 1, 2), source)


def as_lanes(column):
    rows = column.shape[0]
    wide = jnp.broadcast_to(column, (rows, BLOCK))
    return jnp.transpose(wide)[0:1, :]


def regrid(slot_ref, target_ref, source_ref, weight_ref, area_ref, out_ref, mass_ref):
    step = pl.program_id(0)

    @pl.when(step == 0)
    def _():
        out_ref[...] = jnp.zeros_like(out_ref)

    for i in range(PAIRS):
        pair = step * PAIRS + i
        target = pl.multiple_of(target_ref[pair] * BLOCK, BLOCK)
        columns = pl.ds(target, BLOCK)
        product = jnp.dot(
            source_ref[slot_ref[pair]], weight_ref[i], preferred_element_type=jnp.float32
        )
        out_ref[:, columns] += product

    @pl.when(step == pl.num_programs(0) - 1)
    def _():
        rows, cells = out_ref.shape
        total = jnp.zeros((rows, BLOCK), jnp.float32)
        for t in range(cells // BLOCK):
            columns = pl.ds(t * BLOCK, BLOCK)
            total += out_ref[:, columns] * area_ref[:, columns]
        mass_ref[...] = as_lanes(jnp.sum(total, axis=1, keepdims=True))


def regridded_blocks(pair_slot, pair_target, inbound, weights, area):
    slots, rows, _ = inbound.shape
    cells = area.shape[1]
    pairs = weights.shape[0]
    return pl.pallas_call(
        regrid,
        out_shape=(
            jax.ShapeDtypeStruct((rows, cells), jnp.float32),
            jax.ShapeDtypeStruct((1, rows), jnp.float32),
        ),
        grid_spec=pltpu.PrefetchScalarGridSpec(
            num_scalar_prefetch=2,
            grid=(pairs // PAIRS,),
            in_specs=[
                pl.BlockSpec((slots, rows, BLOCK), lambda i, s, t: (0, 0, 0)),
                pl.BlockSpec((PAIRS, BLOCK, BLOCK), lambda i, s, t: (i, 0, 0)),
                pl.BlockSpec((1, cells), lambda i, s, t: (0, 0)),
            ],
            out_specs=(
                pl.BlockSpec((rows, cells), lambda i, s, t: (0, 0)),
                pl.BlockSpec((1, rows), lambda i, s, t: (0, 0)),
            ),
        ),
    )(pair_slot, pair_target, inbound, weights, area)


def exchange(own_ref, sum_ref, all_ref, send_sem, recv_sem):
    here = [lax.axis_index(axis) for axis in AXES]
    sizes = SIZES
    me = ((here[0] * sizes[1] + here[1]) * sizes[2] + here[2]) * sizes[3] + here[3]
    peers = sizes[0] * sizes[1] * sizes[2] * sizes[3]

    def place(step):
        peer = lax.rem(me + step, peers)
        x = lax.rem(peer, sizes[3])
        y = lax.rem(peer // sizes[3], sizes[2])
        core = lax.rem(peer // (sizes[3] * sizes[2]), sizes[1])
        z = peer // (sizes[3] * sizes[2] * sizes[1])
        return (z, core, y, x)

    barrier = pltpu.get_barrier_semaphore()

    def greet(step, _):
        pl.semaphore_signal(
            barrier, inc=1, device_id=place(step), device_id_type=pl.DeviceIdType.MESH
        )
        return 0

    lax.fori_loop(1, peers, greet, 0)
    pl.semaphore_wait(barrier, peers - 1)

    def copy(step):
        return pltpu.make_async_remote_copy(
            src_ref=own_ref,
            dst_ref=all_ref.at[step],
            send_sem=send_sem.at[step],
            recv_sem=recv_sem.at[step],
            device_id=place(step),
            device_id_type=pl.DeviceIdType.MESH,
        )

    def send(step, _):
        copy(step).start()
        return 0

    lax.fori_loop(1, peers, send, 0)

    def arrive(step, _):
        copy(step).wait()
        return 0

    lax.fori_loop(1, peers, arrive, 0)
    total = own_ref[...]
    for step in range(1, peers):
        total += all_ref[step]
    sum_ref[...] = total


def summed(own):
    peers = SIZES[0] * SIZES[1] * SIZES[2] * SIZES[3]
    return pl.pallas_call(
        exchange,
        out_shape=jax.ShapeDtypeStruct(own.shape, own.dtype),
        in_specs=[pl.BlockSpec(memory_space=pltpu.VMEM)],
        out_specs=pl.BlockSpec(memory_space=pltpu.VMEM),
        scratch_shapes=[
            pltpu.VMEM((peers,) + own.shape, own.dtype),
            pltpu.SemaphoreType.DMA((peers,)),
            pltpu.SemaphoreType.DMA((peers,)),
        ],
        compiler_params=pltpu.CompilerParams(collective_id=1, has_side_effects=True),
    )(own)


def shards(src_field, src_area, tgt_area, weights, send_index, pair_slot, pair_target):
    rows = src_field.shape[0]
    peers, capacity = send_index.shape[1:]
    source_local = jnp.sum(src_field.astype(jnp.float32) * src_area[None, :], axis=1)
    outbound = outbound_blocks(send_index, src_field)
    outbound = outbound.reshape(peers, capacity, rows, BLOCK)
    inbound = lax.all_to_all(outbound, AXES, split_axis=0, concat_axis=0, tiled=True)
    inbound = inbound.reshape(peers * capacity, rows, BLOCK)
    regridded, target_local = regridded_blocks(
        pair_slot, pair_target, inbound, weights, tgt_area[None, :]
    )
    own = jnp.concatenate([source_local[None, :], target_local], axis=1)
    total = summed(own)
    scale = total[0, :rows] / total[0, rows:]
    return regridded * scale[:, None]


def solution(mesh):
    split = Mesh(mesh.devices.reshape(SIZES), AXES)
    placed = (
        P(None, AXES),
        P(AXES),
        P(AXES),
        P(AXES, None, None),
        P(AXES, None, None),
        P(AXES),
        P(AXES),
    )
    return jax.shard_map(
        shards, mesh=split, in_specs=placed, out_specs=P(None, AXES), check_vma=False
    )
```

time: 173 us -> 111 us (0.64)
  Pallas kernels: 0 us -> 41.8 us
  other arithmetic: 49.8 us -> 8.34 us
  blocking collectives: 30.5 us -> 0 us
  local copies, waits for them, and re-layouts: 17.5 us -> 0.01 us
  matrix products: 14.4 us -> 0 us
    pallas_call x0 -> x3, Pallas kernels: none -> 41.8 us  [the longest x1 17.9 us: summed(): pl.pallas_call(exchange, out_shape=jax.ShapeDtypeStruct(own.shape, own.dt...]
    scatter-add x1 -> x0, other arithmetic: 39.5 us -> none  [shards(): jax.ops.segment_sum(products, pair_target, num_segments=target_blocks)]
    psum x4 -> x0, blocking collectives: 30.5 us -> none  [by_axis(): value = lax.psum(value, axis)]
    dot_general x1 -> x0, matrix products: 14.4 us -> none  [shards(): jnp.einsum('pcs,pst->pct', picked, weights, preferred_element_type=jnp.fl...]
    gather x2 -> x0, local copies, waits for them, and re-layouts: 11.4 us -> none  [the longest x1 6.17 us: shards(): picked = jnp.take(inbound, pair_slot, axis=0)]
    reshape x1 -> x0, local copies, waits for them, and re-layouts: 5.32 us -> none  [shards(): blocks = src_field.reshape(columns, local_blocks, block_size)]
    select_n x2 -> x0, other arithmetic: 4.03 us -> none  [the longest x1 4.02 us: shards(): outbound = jnp.take(blocks, chosen, axis=1)]
  transfers between devices with their start and end apart: 1 -> 1, of which waited for: 1 -> 1; matrix products, arithmetic and copies ran while one was open for 2% -> 3% of each run, Pallas kernels for 0% -> 0%
where the time goes in v1:
time: 111 us; the launch traced here: 109 us
  waiting for transfers between devices  47.5 us (43%)
  Pallas kernels  41.8 us (38%)
  starting transfers between devices  11.7 us (11%)
  other arithmetic  8.34 us (8%)
    all_to_all x1, waiting for transfers between devices, shards(): lax.all_to_all(outbound, AXES, split_axis=0, concat_axis=0, tiled=True)  47.5 us
    pallas_call x1, Pallas kernels, summed(): pl.pallas_call(exchange, out_shape=jax.ShapeDtypeStruct(own.shape, own.dt...  17.9 us
    pallas_call x1, Pallas kernels, regridded_blocks(): pl.pallas_call(regrid, out_shape=(jax.ShapeDtypeStruct((rows, cells), jnp...  14.7 us
    all_to_all x1, starting transfers between devices, shards(): lax.all_to_all(outbound, AXES, split_axis=0, concat_axis=0, tiled=True)  11.7 us
    pallas_call x1, Pallas kernels, outbound_blocks(): pl.pallas_call(collect, out_shape=jax.ShapeDtypeStruct((slots, rows, BLOC...  9.21 us
    mul x1, other arithmetic, shards(): return regridded * scale[:, None]  3.14 us
    reduce_sum x1, other arithmetic, shards(): jnp.sum(src_field.astype(jnp.float32) * src_area[None, :], axis=1)  3.1 us
  transfers between devices with their start and end apart: 1, of which 1 were waited for; matrix products, arithmetic and copies ran while one was open for 3% of the time, Pallas kernels for 0%

profile of v1, /device:TPU:0, one launch (start us, length us, event | category | flops | bytes accessed | tf_op | source)
XLA Modules:
  0.0 109.4 jit_solution(2603795147380304151)
XLA Ops:
  0.0 9.2 %shard_map.73 = bf16[256,64,128]{2,1,0:T(8,128)(2,1)} custom-call(s32[1,2,128]{2,1,0:T(2,128)} %bitcast.9, bf16[64,32768]{1,0:T(8,128)(2,1)} %source_ref.1), custom_call_target="tpu_custom_call" | custom-call | tf_op jit(solution)/shard_map/pallas_call | solution.py:30
  9.2 0.0 copy-start
  9.2 11.7 %all-to-all-start = ((bf16[128,2,64,128]{3,2,1,0:T(8,128)(2,1)}), bf16[128,2,64,128]{3,2,1,0:T(8,128)(2,1)}, u32[]{:S(2)}, u32[]{:S(2)}) async-start(bf16[128,2,64,128]{3,2,1,0:T(8,128)(2,1)} %bitcast.7), calls=%async_computation | async-start | bytes 8388608 | tf_op jit(solution)/shard_map/all_to_all | solution.py:174
  20.9 0.0 copy-done
  20.9 3.1 %multiply_reduce_fusion = f32[64]{0:T(128)S(1)} fusion(bf16[64,32768]{1,0:T(8,128)(2,1)} %source_ref.1, f32[32768]{0:T(1024)S(1)} %copy-done), kind=kLoop, calls=%fused_computation | loop fusion | flops 6291392 | bytes 4325632 | tf_op jit(solution)/shard_map/reduce_sum | solution.py:171
  24.0 47.5 %all-to-all-done = bf16[128,2,64,128]{3,2,1,0:T(8,128)(2,1)} async-done(((bf16[128,2,64,128]{3,2,1,0:T(8,128)(2,1)}), bf16[128,2,64,128]{3,2,1,0:T(8,128)(2,1)}, u32[]{:S(2)}, u32[]{:S(2)}) %all-to-all-start) | async-done | bytes 4194336 | tf_op jit(solution)/shard_map/all_to_all | solution.py:174
  71.6 14.7 %shard_map.74 = (f32[64,8192]{1,0:T(8,128)}, f32[1,64]{1,0:T(1,128)}) custom-call(s32[384]{0:T(512)} %slot_ref.1, s32[384]{0:T(512)} %target_ref.1, bf16[256,64,128]{2,1,0:T(8,128)(2,1)} %bitcast.2.source_ref, bf16[384,128,128]{2,1,0:T(8,128)(2,1)} %weight_ref.1, f32[1,8192]{1,0:T(1,128)} %bitcast.8), custom_call_target="tpu_custom_call" | custom-call | tf_op jit(solution)/shard_map/pallas_call | solution.py:78
  86.3 1.3 %pad_maximum_fusion.own_ref = f32[1,128]{1,0:T(1,128)} fusion(f32[1,64]{1,0:T(1,128)} %get-tuple-element.8, f32[1,64]{1,0:T(1,128)S(1)} %bitcast.10), kind=kLoop, calls=%fused_computation.2 | loop fusion | flops 128 | bytes 1024 | tf_op jit(solution)/shard_map/concatenate | solution.py:179
  87.5 17.9 %shard_map.75 = f32[1,128]{1,0:T(1,128)} custom-call(f32[1,128]{1,0:T(1,128)} %pad_maximum_fusion.own_ref), custom_call_target="tpu_custom_call" | custom-call | tf_op jit(solution)/shard_map/pallas_call | solution.py:154
  105.4 0.8 fusion
  106.3 3.1 %broadcast_multiply_fusion = f32[64,8192]{1,0:T(8,128)} fusion(f32[64,8192]{1,0:T(8,128)} %get-tuple-element.7, f32[64]{0:T(128)S(1)} %fusion), kind=kLoop, calls=%fused_computation.1 | loop fusion | flops 524288 | bytes 4194560 | tf_op jit(solution)/shard_map/mul | solution.py:182
Async XLA Ops:
  9.2 11.7 %copy-start = (f32[32768]{0:T(1024)S(1)}, f32[32768]{0:T(1024)}, u32[]{:S(2)}) copy-start(f32[32768]{0:T(1024)} %param.8) | copy-start | bytes 393220
  9.2 62.3 %all-to-all-start = ((bf16[128,2,64,128]{3,2,1,0:T(8,128)(2,1)}), bf16[128,2,64,128]{3,2,1,0:T(8,128)(2,1)}, u32[]{:S(2)}, u32[]{:S(2)}) async-start(bf16[128,2,64,128]{3,2,1,0:T(8,128)(2,1)} %bitcast.7), calls=%async_computation | async-start | bytes 8388608 | tf_op jit(solution)/shard_map/all_to_all | solution.py:174

commit v2 on v1

v2 whole, which is shorter than its diff:
```python
import itertools

import jax
import jax.numpy as jnp
from jax import lax
from jax.experimental import pallas as pl
from jax.experimental.pallas import tpu as pltpu
from jax.sharding import Mesh
from jax.sharding import PartitionSpec as P

AXES = ("z", "core", "y", "x")
SIZES = (4, 2, 4, 4)
BLOCK = 128
GATHERED = 32
PAIRS = 32


def collect(index_ref, source_ref, out_ref, held, in_sem, out_sem):
    slots = held.shape[0]
    groups = slots // GATHERED

    def span(group):
        return pl.ds(group * GATHERED, GATHERED)

    for slot in range(slots):
        block = jnp.maximum(index_ref[0, slot % 2, slot // 2], 0)
        columns = pl.ds(pl.multiple_of(block * BLOCK, BLOCK), BLOCK)
        pltpu.make_async_copy(
            source_ref.at[:, columns], held.at[slot], in_sem.at[slot // GATHERED]
        ).start()
    for group in range(groups):
        pltpu.make_async_copy(
            out_ref.at[span(group)], held.at[span(group)], in_sem.at[group]
        ).wait()
        pltpu.make_async_copy(
            held.at[span(group)], out_ref.at[span(group)], out_sem.at[group]
        ).start()
    for group in range(groups):
        pltpu.make_async_copy(
            held.at[span(group)], out_ref.at[span(group)], out_sem.at[group]
        ).wait()


def outbound_blocks(send_index, source):
    rows = source.shape[0]
    peers, capacity = send_index.shape[1:]
    slots = peers * capacity
    return pl.pallas_call(
        collect,
        out_shape=jax.ShapeDtypeStruct((slots, rows, BLOCK), source.dtype),
        in_specs=[
            pl.BlockSpec(memory_space=pltpu.SMEM),
            pl.BlockSpec(memory_space=pl.ANY),
        ],
        out_specs=pl.BlockSpec(memory_space=pl.ANY),
        scratch_shapes=[
            pltpu.VMEM((slots, rows, BLOCK), source.dtype),
            pltpu.SemaphoreType.DMA((slots // GATHERED,)),
            pltpu.SemaphoreType.DMA((slots // GATHERED,)),
        ],
    )(jnp.swapaxes(send_index, 1, 2), source)


def slot_weights(slot_ref, target_ref, area_ref, weight_ref, out_ref, sums, areas):
    step = pl.program_id(0)

    @pl.when(step == 0)
    def _():
        sums[...] = jnp.zeros_like(sums)
        area = area_ref[...]
        high = area.astype(jnp.bfloat16)
        low = (area - high.astype(jnp.float32)).astype(jnp.bfloat16)
        areas[:, 0:8, :] = jnp.broadcast_to(high[:, None, :], (area.shape[0], 8, BLOCK))
        areas[:, 8:16, :] = jnp.broadcast_to(low[:, None, :], (area.shape[0], 8, BLOCK))

    for i in range(PAIRS):
        pair = step * PAIRS + i
        product = lax.dot_general(
            areas[target_ref[pair]],
            weight_ref[i],
            (((1,), (1,)), ((), ())),
            preferred_element_type=jnp.float32,
        )
        sums[slot_ref[pair]] += product[0:8] + product[8:16]

    @pl.when(step == pl.num_programs(0) - 1)
    def _():
        out_ref[...] = sums[:, 0, :]


def weights_of_slots(pair_slot, pair_target, area, weights, slots):
    pairs = weights.shape[0]
    targets = area.shape[0]
    return pl.pallas_call(
        slot_weights,
        out_shape=jax.ShapeDtypeStruct((slots, BLOCK), jnp.float32),
        grid_spec=pltpu.PrefetchScalarGridSpec(
            num_scalar_prefetch=2,
            grid=(pairs // PAIRS,),
            in_specs=[
                pl.BlockSpec((targets, BLOCK), lambda i, s, t: (0, 0)),
                pl.BlockSpec((PAIRS, BLOCK, BLOCK), lambda i, s, t: (i, 0, 0)),
            ],
            out_specs=pl.BlockSpec((slots, BLOCK), lambda i, s, t: (0, 0)),
            scratch_shapes=[
                pltpu.VMEM((slots, 8, BLOCK), jnp.float32),
                pltpu.VMEM((targets, 16, BLOCK), jnp.bfloat16),
            ],
        ),
        cost_estimate=pl.CostEstimate(
            flops=2 * pairs * 64 * BLOCK * BLOCK,
            bytes_accessed=pairs * BLOCK * BLOCK * 2,
            transcendentals=0,
        ),
    )(pair_slot, pair_target, area, weights)


def as_lanes(column):
    rows = column.shape[0]
    wide = jnp.broadcast_to(column, (rows, BLOCK))
    return jnp.transpose(wide)[0:1, :]


def regrid(slot_ref, target_ref, source_ref, weight_ref, total_ref, out_ref):
    step = pl.program_id(0)

    @pl.when(step == 0)
    def _():
        out_ref[...] = jnp.zeros_like(out_ref)

    for i in range(PAIRS):
        pair = step * PAIRS + i
        target = pl.multiple_of(target_ref[pair] * BLOCK, BLOCK)
        columns = pl.ds(target, BLOCK)
        product = jnp.dot(
            source_ref[slot_ref[pair]], weight_ref[i], preferred_element_type=jnp.float32
        )
        out_ref[:, columns] += product

    @pl.when(step == pl.num_programs(0) - 1)
    def _():
        rows, cells = out_ref.shape
        total = jnp.transpose(jnp.broadcast_to(total_ref[...], (BLOCK, BLOCK)))
        scale = total[:rows] / total[rows : 2 * rows]
        for t in range(cells // BLOCK):
            columns = pl.ds(t * BLOCK, BLOCK)
            out_ref[:, columns] = out_ref[:, columns] * scale


def target_blocks(pair_slot, pair_target, inbound, weights, total, cells):
    slots, rows, _ = inbound.shape
    pairs = weights.shape[0]
    return pl.pallas_call(
        regrid,
        out_shape=jax.ShapeDtypeStruct((rows, cells), jnp.float32),
        grid_spec=pltpu.PrefetchScalarGridSpec(
            num_scalar_prefetch=2,
            grid=(pairs // PAIRS,),
            in_specs=[
                pl.BlockSpec((slots, rows, BLOCK), lambda i, s, t: (0, 0, 0)),
                pl.BlockSpec((PAIRS, BLOCK, BLOCK), lambda i, s, t: (i, 0, 0)),
                pl.BlockSpec((1, BLOCK), lambda i, s, t: (0, 0)),
            ],
            out_specs=pl.BlockSpec((rows, cells), lambda i, s, t: (0, 0)),
        ),
    )(pair_slot, pair_target, inbound, weights, total)


def masses(
    slot_ref, source_ref, block_ref, total_ref,
    back, own, others, send_sem, back_sem, mass_send_sem, mass_sem,
):
    here = [lax.axis_index(axis) for axis in AXES]
    turned = [[lax.rem(h + k, size) for k in range(size)] for h, size in zip(here, SIZES)]
    peers = SIZES[0] * SIZES[1] * SIZES[2] * SIZES[3]

    def number(place):
        value = place[0]
        for size, part in zip(SIZES[1:], place[1:]):
            value = value * size + part
        return value

    places = [
        tuple(axis[k] for axis, k in zip(turned, offset))
        for offset in itertools.product(*(range(size) for size in SIZES))
    ][1:]
    me = number(here)
    barrier = pltpu.get_barrier_semaphore()
    for place in places:
        pl.semaphore_signal(
            barrier, inc=1, device_id=place, device_id_type=pl.DeviceIdType.MESH
        )
    pl.semaphore_wait(barrier, peers - 1)
    for place in places:
        pltpu.make_async_remote_copy(
            src_ref=slot_ref.at[number(place)],
            dst_ref=back.at[me],
            send_sem=send_sem,
            recv_sem=back_sem,
            device_id=place,
            device_id_type=pl.DeviceIdType.MESH,
        ).start()
    back[me] = slot_ref[me]
    most = pl.ds(0, peers - 1)
    pltpu.make_async_copy(slot_ref.at[most], back.at[most], back_sem).wait()
    pltpu.make_async_copy(slot_ref.at[most], back.at[most], send_sem).wait()
    rows = block_ref.shape[2]

    def add(peer, total):
        for slot in range(block_ref.shape[1]):
            factors = back[peer, pl.ds(slot, 1), :]
            total += block_ref[peer, slot].astype(jnp.float32) * factors
        return total

    total = lax.fori_loop(0, peers, add, jnp.zeros((rows, BLOCK), jnp.float32), unroll=4)
    target = as_lanes(jnp.sum(total, axis=1, keepdims=True))
    own[...] = jnp.concatenate([source_ref[...], target], axis=1)
    others[me] = own[...]
    for place in places:
        pltpu.make_async_remote_copy(
            src_ref=own,
            dst_ref=others.at[me],
            send_sem=mass_send_sem,
            recv_sem=mass_sem,
            device_id=place,
            device_id_type=pl.DeviceIdType.MESH,
        ).start()
    pltpu.make_async_copy(others.at[most], others.at[most], mass_sem).wait()
    pltpu.make_async_copy(others.at[most], others.at[most], mass_send_sem).wait()
    total = others[0]
    for peer in range(1, peers):
        total += others[peer]
    total_ref[...] = total


def total_masses(slot_sums, source_local, outbound):
    peers, capacity, rows, _ = outbound.shape
    return pl.pallas_call(
        masses,
        out_shape=jax.ShapeDtypeStruct((1, 2 * rows), jnp.float32),
        in_specs=[pl.BlockSpec(memory_space=pltpu.VMEM)] * 3,
        out_specs=pl.BlockSpec(memory_space=pltpu.VMEM),
        scratch_shapes=[
            pltpu.VMEM((peers, capacity, BLOCK), jnp.float32),
            pltpu.VMEM((1, 2 * rows), jnp.float32),
            pltpu.VMEM((peers, 1, 2 * rows), jnp.float32),
        ]
        + [pltpu.SemaphoreType.DMA] * 4,
        compiler_params=pltpu.CompilerParams(collective_id=1, has_side_effects=True),
        cost_estimate=pl.CostEstimate(
            flops=2 * 400 * 64 * BLOCK * BLOCK, bytes_accessed=4194304, transcendentals=0
        ),
    )(slot_sums, source_local, outbound)


def shards(src_field, src_area, tgt_area, weights, send_index, pair_slot, pair_target):
    rows = src_field.shape[0]
    peers, capacity = send_index.shape[1:]
    source_local = jnp.sum(src_field.astype(jnp.float32) * src_area[None, :], axis=1)
    outbound = outbound_blocks(send_index, src_field)
    outbound = outbound.reshape(peers, capacity, rows, BLOCK)
    slot_sums = weights_of_slots(
        pair_slot, pair_target, tgt_area.reshape(-1, BLOCK), weights, peers * capacity
    )
    slot_sums = slot_sums.reshape(peers, capacity, BLOCK)
    total = total_masses(slot_sums, source_local[None, :], outbound)
    inbound = lax.all_to_all(outbound, AXES, split_axis=0, concat_axis=0, tiled=True)
    inbound = inbound.reshape(peers * capacity, rows, BLOCK)
    return target_blocks(
        pair_slot, pair_target, inbound, weights, total, tgt_area.shape[0]
    )


def solution(mesh):
    split = Mesh(mesh.devices.reshape(SIZES), AXES)
    placed = (
        P(None, AXES),
        P(AXES),
        P(AXES),
        P(AXES, None, None),
        P(AXES, None, None),
        P(AXES),
        P(AXES),
    )
    return jax.shard_map(
        shards, mesh=split, in_specs=placed, out_specs=P(None, AXES), check_vma=False
    )
```

time: 111 us -> 96.7 us (0.87)
  waiting for transfers between devices: 47.5 us -> 0.01 us
  Pallas kernels: 41.8 us -> 79.5 us
  other arithmetic: 8.34 us -> 3.62 us
    all_to_all x1, waiting for transfers between devices: 47.5 us -> 0.01 us  [shards(): lax.all_to_all(outbound, AXES, split_axis=0, concat_axis=0, tiled=True)]
    pallas_call x2 -> x3, Pallas kernels: 32.6 us -> 71.4 us  [the longest x1 42.6 us: total_masses(): pl.pallas_call(masses, out_shape=jax.ShapeDtypeStruct((1, 2 * rows), jnp....]
    mul x1 -> x0, other arithmetic: 3.14 us -> none  [shards(): return regridded * scale[:, None]]
    concatenate x1 -> x0, other arithmetic: 1.28 us -> none  [shards(): own = jnp.concatenate([source_local[None, :], target_local], axis=1)]
  transfers between devices with their start and end apart: 1 -> 1, of which waited for: 1 -> 0; matrix products, arithmetic and copies ran while one was open for 3% -> 4% of each run, Pallas kernels for 0% -> 60%
where the time goes in v2:
time: 96.7 us; the launch traced here: 94.9 us
  Pallas kernels  79.5 us (82%)
  starting transfers between devices  11.7 us (12%)
  other arithmetic  3.62 us (4%)
    pallas_call x1, Pallas kernels, total_masses(): pl.pallas_call(masses, out_shape=jax.ShapeDtypeStruct((1, 2 * rows), jnp....  42.6 us
    pallas_call x1, Pallas kernels, target_blocks(): pl.pallas_call(regrid, out_shape=jax.ShapeDtypeStruct((rows, cells), jnp....  14.7 us
    pallas_call x1, Pallas kernels, weights_of_slots(): pl.pallas_call(slot_weights, out_shape=jax.ShapeDtypeStruct((slots, BLOCK...  14.1 us
    all_to_all x1, starting transfers between devices, shards(): lax.all_to_all(outbound, AXES, split_axis=0, concat_axis=0, tiled=True)  11.7 us
    pallas_call x1, Pallas kernels, outbound_blocks(): pl.pallas_call(collect, out_shape=jax.ShapeDtypeStruct((slots, rows, BLOC...  8.12 us
    reduce_sum x1, other arithmetic, shards(): jnp.sum(src_field.astype(jnp.float32) * src_area[None, :], axis=1)  3.62 us
  transfers between devices with their start and end apart: 1, of which 0 were waited for; matrix products, arithmetic and copies ran while one was open for 4% of the time, Pallas kernels for 60%

profile of v2, /device:TPU:0, one launch (start us, length us, event | category | flops | bytes accessed | tf_op | source)
XLA Modules:
  0.0 94.9 jit_solution(5239744685333196771)
XLA Ops:
  0.0 8.1 %shard_map.73 = bf16[256,64,128]{2,1,0:T(8,128)(2,1)} custom-call(s32[1,2,128]{2,1,0:T(2,128)} %bitcast.11, bf16[64,32768]{1,0:T(8,128)(2,1)} %source_ref.1), custom_call_target="tpu_custom_call" | custom-call | tf_op jit(solution)/shard_map/pallas_call | solution.py:48
  8.1 11.7 %all-to-all-start = ((bf16[128,2,64,128]{3,2,1,0:T(8,128)(2,1)}), bf16[128,2,64,128]{3,2,1,0:T(8,128)(2,1)}, u32[]{:S(2)}, u32[]{:S(2)}) async-start(bf16[128,2,64,128]{3,2,1,0:T(8,128)(2,1)} %bitcast.6), calls=%async_computation | async-start | bytes 8388608 | tf_op jit(solution)/shard_map/all_to_all | solution.py:267
  19.9 0.0 copy-start
  19.9 14.1 %shard_map.74 = f32[256,128]{1,0:T(8,128)} custom-call(s32[384]{0:T(512)} %slot_ref.3, s32[384]{0:T(512)} %target_ref.3, f32[64,128]{1,0:T(8,128)} %bitcast.9, bf16[384,128,128]{2,1,0:T(8,128)(2,1)} %weight_ref.3), custom_call_target="tpu_custom_call" | custom-call | flops 805306368 | bytes 12582912 | tf_op jit(solution)/shard_map/pallas_call | solution.py:94
  34.0 0.0 copy-done
  34.0 3.6 %multiply_reduce_fusion = f32[64]{0:T(128)} fusion(bf16[64,32768]{1,0:T(8,128)(2,1)} %source_ref.1, f32[32768]{0:T(1024)S(1)} %copy-done), kind=kLoop, calls=%fused_computation | loop fusion | flops 6291392 | bytes 4325632 | tf_op jit(solution)/shard_map/reduce_sum | solution.py:259
  37.6 42.6 %shard_map.75.total_ref = f32[1,128]{1,0:T(1,128)} custom-call(f32[128,2,128]{2,1,0:T(2,128)} %bitcast.8, f32[1,64]{1,0:T(1,128)} %bitcast.10, bf16[128,2,64,128]{3,2,1,0:T(8,128)(2,1)} %bitcast.7), custom_call_target="tpu_custom_call" | custom-call | flops 838860800 | bytes 4194304 | tf_op jit(solution)/shard_map/pallas_call | solution.py:238
  80.3 0.0 all-to-all-done
  80.3 14.7 %shard_map.76 = f32[64,8192]{1,0:T(8,128)} custom-call(s32[384]{0:T(512)} %slot_ref.3, s32[384]{0:T(512)} %target_ref.3, bf16[256,64,128]{2,1,0:T(8,128)(2,1)} %bitcast.2.source_ref, bf16[384,128,128]{2,1,0:T(8,128)(2,1)} %weight_ref.3, f32[1,128]{1,0:T(1,128)} %shard_map.75.total_ref), custom_call_target="tpu_custom_call" | custom-call | tf_op jit(solution)/shard_map/pallas_call | solution.py:153
Async XLA Ops:
  8.1 72.1 %all-to-all-start = ((bf16[128,2,64,128]{3,2,1,0:T(8,128)(2,1)}), bf16[128,2,64,128]{3,2,1,0:T(8,128)(2,1)}, u32[]{:S(2)}, u32[]{:S(2)}) async-start(bf16[128,2,64,128]{3,2,1,0:T(8,128)(2,1)} %bitcast.6), calls=%async_computation | async-start | bytes 8388608 | tf_op jit(solution)/shard_map/all_to_all | solution.py:267
  19.9 14.1 %copy-start = (f32[32768]{0:T(1024)S(1)}, f32[32768]{0:T(1024)}, u32[]{:S(2)}) copy-start(f32[32768]{0:T(1024)} %param.8) | copy-start | bytes 393220

commit v3 on v0

v3 whole, which is shorter than its diff:
```python
import itertools

import jax
import jax.numpy as jnp
from jax import lax
from jax.experimental import pallas as pl
from jax.experimental.pallas import tpu as pltpu
from jax.sharding import Mesh
from jax.sharding import PartitionSpec as P

AXES = ("z", "core", "y", "x")
SIZES = (4, 2, 4, 4)
PEERS = 128
BLOCK = 128
GATHERED = 32
PAIRS = 32
EARLY = 40
MESH = pl.DeviceIdType.MESH
ANY = pl.BlockSpec(memory_space=pl.ANY)
SMEM = pl.BlockSpec(memory_space=pltpu.SMEM)
VMEM = pl.BlockSpec(memory_space=pltpu.VMEM)


def chunk(index, size):
    return pl.ds(pl.multiple_of(index * size, size), size)


def prepare(
    index_ref, slot_ref, target_ref, area_ref, source_ref, weight_ref, out_ref, sum_ref,
    held, weights, sums, areas, in_sem, out_sem, weight_sem,
):
    slots = held.shape[0]
    pairs = weights.shape[0]

    for slot in range(slots):
        block = jnp.maximum(index_ref[0, slot % 2, slot // 2], 0)
        columns = pl.ds(pl.multiple_of(block * BLOCK, BLOCK), BLOCK)
        pltpu.make_async_copy(
            source_ref.at[:, columns], held.at[slot], in_sem.at[slot // GATHERED]
        ).start()
    for part in range(pairs // PAIRS):
        span = pl.ds(part * PAIRS, PAIRS)
        pltpu.make_async_copy(
            weight_ref.at[span], weights.at[span], weight_sem.at[part]
        ).start()
    sums[...] = jnp.zeros_like(sums)
    area = area_ref[...]
    high = area.astype(jnp.bfloat16)
    low = (area - high.astype(jnp.float32)).astype(jnp.bfloat16)
    areas[:, 0:8, :] = jnp.broadcast_to(high[:, None, :], (area.shape[0], 8, BLOCK))
    areas[:, 8:16, :] = jnp.broadcast_to(low[:, None, :], (area.shape[0], 8, BLOCK))
    for group in range(slots // GATHERED):
        span = pl.ds(group * GATHERED, GATHERED)
        pltpu.make_async_copy(out_ref.at[span], held.at[span], in_sem.at[group]).wait()
        pltpu.make_async_copy(held.at[span], out_ref.at[span], out_sem.at[group]).start()

    def part_of(part, _):
        span = chunk(part, PAIRS)
        pltpu.make_async_copy(
            weight_ref.at[span], weights.at[span], weight_sem.at[part]
        ).wait()
        for i in range(PAIRS):
            pair = part * PAIRS + i
            product = lax.dot_general(
                areas[target_ref[pair]],
                weights[pair],
                (((1,), (1,)), ((), ())),
                preferred_element_type=jnp.float32,
            )
            sums[slot_ref[pair]] += product[0:8] + product[8:16]
        return 0

    lax.fori_loop(0, pairs // PAIRS, part_of, 0)
    sum_ref[...] = sums[:, 0, :]
    for group in range(slots // GATHERED):
        span = pl.ds(group * GATHERED, GATHERED)
        pltpu.make_async_copy(held.at[span], out_ref.at[span], out_sem.at[group]).wait()


def prepared(send_index, pair_slot, pair_target, area, source, weights):
    rows = source.shape[0]
    peers, capacity = send_index.shape[1:]
    slots = peers * capacity
    targets = area.shape[0]
    pairs = weights.shape[0]
    return pl.pallas_call(
        prepare,
        out_shape=(
            jax.ShapeDtypeStruct((slots, rows, BLOCK), source.dtype),
            jax.ShapeDtypeStruct((slots, BLOCK), jnp.float32),
        ),
        in_specs=[SMEM, SMEM, SMEM, VMEM, ANY, ANY],
        out_specs=(ANY, VMEM),
        scratch_shapes=[
            pltpu.VMEM((slots, rows, BLOCK), source.dtype),
            pltpu.VMEM(weights.shape, weights.dtype),
            pltpu.VMEM((slots, 8, BLOCK), jnp.float32),
            pltpu.VMEM((targets, 16, BLOCK), jnp.bfloat16),
            pltpu.SemaphoreType.DMA((slots // GATHERED,)),
            pltpu.SemaphoreType.DMA((slots // GATHERED,)),
            pltpu.SemaphoreType.DMA((pairs // PAIRS,)),
        ],
    )(jnp.swapaxes(send_index, 1, 2), pair_slot, pair_target, area, source, weights)


def as_lanes(column):
    rows = column.shape[0]
    wide = jnp.broadcast_to(column, (rows, BLOCK))
    return jnp.transpose(wide)[0:1, :]


def routes():
    left = [offset for offset in itertools.product(*(range(size) for size in SIZES))][1:]

    def load(offset):
        links = [0] * 6
        for axis, step in enumerate((offset[0], offset[2], offset[3])):
            links[2 * axis] += step in (1, 2)
            links[2 * axis + 1] += step in (2, 3)
        return links

    used = [0] * 6
    order = []
    while left:
        def spread(offset):
            after = [a + b for a, b in zip(used, load(offset))]
            return max(after) - min(after)

        best = min(left, key=spread)
        left.remove(best)
        used = [a + b for a, b in zip(used, load(best))]
        order.append(best)
    return order


def exchange(
    slot_ref, source_ref, area_ref, block_ref, in_ref, total_ref,
    back, own, others, blocks, source,
    send_sem, recv_sem, near_sem, block_sem, source_sem,
    back_send_sem, back_sem, mass_send_sem, mass_sem,
):
    here = [lax.axis_index(axis) for axis in AXES]
    turned = [[lax.rem(h + k, size) for k in range(size)] for h, size in zip(here, SIZES)]

    def number(place):
        value = place[0]
        for size, part in zip(SIZES[1:], place[1:]):
            value = value * size + part
        return value

    places = [
        tuple(axis[k] for axis, k in zip(turned, offset)) for offset in routes()
    ]
    me = number(here)
    capacity, rows = block_ref.shape[1:3]
    barrier = pltpu.get_barrier_semaphore()
    for place in places:
        pl.semaphore_signal(barrier, inc=1, device_id=place, device_id_type=MESH)
    near = pltpu.make_async_copy(block_ref, blocks, block_sem)
    near.start()
    far = pltpu.make_async_copy(source_ref, source, source_sem)
    far.start()
    back[me] = slot_ref[me]
    pl.semaphore_wait(barrier, PEERS - 1)

    for place in places:
        pltpu.make_async_remote_copy(
            src_ref=slot_ref.at[number(place)],
            dst_ref=back.at[me],
            send_sem=back_send_sem,
            recv_sem=back_sem,
            device_id=place,
            device_id_type=MESH,
        ).start()

    def send(place):
        pltpu.make_async_remote_copy(
            src_ref=block_ref.at[number(place)],
            dst_ref=in_ref.at[me],
            send_sem=send_sem,
            recv_sem=recv_sem,
            device_id=place,
            device_id_type=MESH,
        ).start()

    for place in places[:EARLY]:
        send(place)

    near.wait()
    kept = pltpu.make_async_copy(blocks.at[me], in_ref.at[me], near_sem)
    kept.start()
    far.wait()

    def source_part(part, total):
        columns = chunk(part, BLOCK)
        return total + source[:, columns].astype(jnp.float32) * area_ref[:, columns]

    zero = jnp.zeros((rows, BLOCK), jnp.float32)
    count = source.shape[1] // BLOCK
    source_total = lax.fori_loop(0, count, source_part, zero, unroll=8)
    most = pl.ds(0, PEERS - 1)
    pltpu.make_async_copy(slot_ref.at[most], back.at[most], back_sem).wait()

    def target_part(peer, total):
        for slot in range(capacity):
            factors = back[peer, pl.ds(slot, 1), :]
            total += blocks[peer, slot].astype(jnp.float32) * factors
        return total

    target_total = lax.fori_loop(0, PEERS, target_part, zero, unroll=4)
    column = jnp.concatenate(
        [
            jnp.sum(source_total, axis=1, keepdims=True),
            jnp.sum(target_total, axis=1, keepdims=True),
        ],
        axis=0,
    )
    own[...] = as_lanes(column)
    others[me] = own[...]
    for place in places:
        pltpu.make_async_remote_copy(
            src_ref=own,
            dst_ref=others.at[me],
            send_sem=mass_send_sem,
            recv_sem=mass_sem,
            device_id=place,
            device_id_type=MESH,
        ).start()
    for place in places[EARLY:]:
        send(place)
    pltpu.make_async_copy(others.at[most], others.at[most], mass_sem).wait()
    total = others[0]
    for peer in range(1, PEERS):
        total += others[peer]
    total_ref[...] = total
    pltpu.make_async_copy(others.at[most], others.at[most], mass_send_sem).wait()
    pltpu.make_async_copy(slot_ref.at[most], back.at[most], back_send_sem).wait()
    kept.wait()
    pltpu.make_async_copy(block_ref.at[most], in_ref.at[most], send_sem).wait()
    pltpu.make_async_copy(block_ref.at[most], in_ref.at[most], recv_sem).wait()


def exchanged(slot_sums, source, area, outbound):
    peers, capacity, rows, _ = outbound.shape
    return pl.pallas_call(
        exchange,
        out_shape=(
            jax.ShapeDtypeStruct(outbound.shape, outbound.dtype),
            jax.ShapeDtypeStruct((1, 2 * rows), jnp.float32),
        ),
        in_specs=[VMEM, ANY, VMEM, ANY],
        out_specs=(ANY, VMEM),
        scratch_shapes=[
            pltpu.VMEM((peers, capacity, BLOCK), jnp.float32),
            pltpu.VMEM((1, 2 * rows), jnp.float32),
            pltpu.VMEM((peers, 1, 2 * rows), jnp.float32),
            pltpu.VMEM(outbound.shape, outbound.dtype),
            pltpu.VMEM(source.shape, source.dtype),
        ]
        + [pltpu.SemaphoreType.DMA] * 9,
        compiler_params=pltpu.CompilerParams(collective_id=1, has_side_effects=True),
    )(slot_sums, source, area, outbound)


def regrid(
    slot_ref, target_ref, total_ref, source_ref, weight_ref, out_ref,
    source, weights, source_sem, weight_sem,
):
    pairs = weights.shape[0]
    far = pltpu.make_async_copy(source_ref, source, source_sem)
    far.start()
    for part in range(pairs // PAIRS):
        span = pl.ds(part * PAIRS, PAIRS)
        pltpu.make_async_copy(
            weight_ref.at[span], weights.at[span], weight_sem.at[part]
        ).start()
    out_ref[...] = jnp.zeros_like(out_ref)
    far.wait()

    def part_of(part, _):
        span = chunk(part, PAIRS)
        pltpu.make_async_copy(
            weight_ref.at[span], weights.at[span], weight_sem.at[part]
        ).wait()
        for i in range(PAIRS):
            pair = part * PAIRS + i
            product = jnp.dot(
                source[slot_ref[pair]], weights[pair], preferred_element_type=jnp.float32
            )
            out_ref[:, chunk(target_ref[pair], BLOCK)] += product
        return 0

    lax.fori_loop(0, pairs // PAIRS, part_of, 0)
    rows, cells = out_ref.shape
    total = jnp.transpose(jnp.broadcast_to(total_ref[...], (BLOCK, BLOCK)))
    scale = total[:rows] / total[rows : 2 * rows]
    for t in range(cells // BLOCK):
        columns = pl.ds(t * BLOCK, BLOCK)
        out_ref[:, columns] = out_ref[:, columns] * scale


def target_blocks(pair_slot, pair_target, inbound, weights, total, cells):
    slots, rows, _ = inbound.shape
    pairs = weights.shape[0]
    return pl.pallas_call(
        regrid,
        out_shape=jax.ShapeDtypeStruct((rows, cells), jnp.float32),
        in_specs=[SMEM, SMEM, VMEM, ANY, ANY],
        out_specs=VMEM,
        scratch_shapes=[
            pltpu.VMEM(inbound.shape, inbound.dtype),
            pltpu.VMEM(weights.shape, weights.dtype),
            pltpu.SemaphoreType.DMA,
            pltpu.SemaphoreType.DMA((pairs // PAIRS,)),
        ],
    )(pair_slot, pair_target, total, inbound, weights)


def shards(src_field, src_area, tgt_area, weights, send_index, pair_slot, pair_target):
    rows = src_field.shape[0]
    peers, capacity = send_index.shape[1:]
    outbound, slot_sums = prepared(
        send_index, pair_slot, pair_target, tgt_area.reshape(-1, BLOCK), src_field, weights
    )
    inbound, total = exchanged(
        slot_sums.reshape(peers, capacity, BLOCK),
        src_field,
        src_area[None, :],
        outbound.reshape(peers, capacity, rows, BLOCK),
    )
    inbound = inbound.reshape(peers * capacity, rows, BLOCK)
    return target_blocks(
        pair_slot, pair_target, inbound, weights, total, tgt_area.shape[0]
    )


def solution(mesh):
    split = Mesh(mesh.devices.reshape(SIZES), AXES)
    placed = (
        P(None, AXES),
        P(AXES),
        P(AXES),
        P(AXES, None, None),
        P(AXES, None, None),
        P(AXES),
        P(AXES),
    )
    return jax.shard_map(
        shards, mesh=split, in_specs=placed, out_specs=P(None, AXES), check_vma=False
    )
```

time: 173 us -> 95.1 us (0.55)
  Pallas kernels: 0 us -> 94.1 us
  other arithmetic: 49.8 us -> 0 us
  waiting for transfers between devices: 47.5 us -> 0 us
  blocking collectives: 30.5 us -> 0 us
  local copies, waits for them, and re-layouts: 17.5 us -> 0 us
  matrix products: 14.4 us -> 0 us
  starting transfers between devices: 11.7 us -> 0 us
    pallas_call x0 -> x3, Pallas kernels: none -> 94.1 us  [the longest x1 62.5 us: exchanged(): pl.pallas_call(exchange, out_shape=(jax.ShapeDtypeStruct(outbound.shape,...]
    all_to_all x1 -> x0, waiting for transfers between devices: 47.5 us -> none  [shards(): lax.all_to_all(outbound, ROW_COL, split_axis=0, concat_axis=0, tiled=True)]
    scatter-add x1 -> x0, other arithmetic: 39.5 us -> none  [shards(): jax.ops.segment_sum(products, pair_target, num_segments=target_blocks)]
    psum x4 -> x0, blocking collectives: 30.5 us -> none  [by_axis(): value = lax.psum(value, axis)]
    dot_general x1 -> x0, matrix products: 14.4 us -> none  [shards(): jnp.einsum('pcs,pst->pct', picked, weights, preferred_element_type=jnp.fl...]
    all_to_all x1 -> x0, starting transfers between devices: 11.7 us -> none  [shards(): lax.all_to_all(outbound, ROW_COL, split_axis=0, concat_axis=0, tiled=True)]
    gather x2 -> x0, local copies, waits for them, and re-layouts: 11.4 us -> none  [the longest x1 6.17 us: shards(): picked = jnp.take(inbound, pair_slot, axis=0)]
    reshape x1 -> x0, local copies, waits for them, and re-layouts: 5.32 us -> none  [shards(): blocks = src_field.reshape(columns, local_blocks, block_size)]
  transfers between devices with their start and end apart: 1 -> 0, of which waited for: 1 -> 0; matrix products, arithmetic and copies ran while one was open for 2% -> 0% of each run, Pallas kernels for 0% -> 0%
where the time goes in v3:
time: 95.1 us; the launch traced here: 94.1 us
  Pallas kernels  94.1 us (99%)
    pallas_call x1, Pallas kernels, exchanged(): pl.pallas_call(exchange, out_shape=(jax.ShapeDtypeStruct(outbound.shape,...  62.5 us
    pallas_call x1, Pallas kernels, prepared(): pl.pallas_call(prepare, out_shape=(jax.ShapeDtypeStruct((slots, rows, BLO...  18.3 us
    pallas_call x1, Pallas kernels, target_blocks(): pl.pallas_call(regrid, out_shape=jax.ShapeDtypeStruct((rows, cells), jnp....  13.3 us

profile of v3, /device:TPU:0, one launch (start us, length us, event | category | flops | bytes accessed | tf_op | source)
XLA Modules:
  0.0 94.1 jit_solution(12720064864655880578)
XLA Ops:
  0.0 18.3 %shard_map.73 = (bf16[256,64,128]{2,1,0:T(8,128)(2,1)}, f32[256,128]{1,0:T(8,128)}) custom-call(s32[1,2,128]{2,1,0:T(2,128)} %bitcast.11, s32[384]{0:T(512)} %slot_ref.3, s32[384]{0:T(512)} %target_ref.3, f32[64,128]{1,0:T(8,128)} %bitcast.10, bf16[64,32768]{1,0:T(8,128)(2,1)} %source_ref.3, bf16[384,128,128]{2,1,0:T(8,128)(2,1)} %weight_ref.3), custom_call_target="tpu_custom_call" | custom-call | tf_op jit(solution)/shard_map/pallas_call | solution.py:86
  18.3 62.5 %shard_map.74 = (bf16[128,2,64,128]{3,2,1,0:T(8,128)(2,1)}, f32[1,128]{1,0:T(1,128)}) custom-call(f32[128,2,128]{2,1,0:T(2,128)} %bitcast.9, bf16[64,32768]{1,0:T(8,128)(2,1)} %source_ref.3, f32[1,32768]{1,0:T(1,128)} %bitcast.8, bf16[128,2,64,128]{3,2,1,0:T(8,128)(2,1)} %bitcast.6), custom_call_target="tpu_custom_call" | custom-call | tf_op jit(solution)/shard_map/pallas_call | solution.py:245
  80.8 13.3 %shard_map.75 = f32[64,8192]{1,0:T(8,128)} custom-call(s32[384]{0:T(512)} %slot_ref.3, s32[384]{0:T(512)} %target_ref.3, f32[1,128]{1,0:T(1,128)} %get-tuple-element.11.total_ref, bf16[256,64,128]{2,1,0:T(8,128)(2,1)} %bitcast.7, bf16[384,128,128]{2,1,0:T(8,128)(2,1)} %weight_ref.3), custom_call_target="tpu_custom_call" | custom-call | tf_op jit(solution)/shard_map/pallas_call | solution.py:305

commit v4 on v3

v4 whole, which is shorter than its diff:
```python
import itertools

import jax
import jax.numpy as jnp
from jax import lax
from jax.experimental import pallas as pl
from jax.experimental.pallas import tpu as pltpu
from jax.sharding import Mesh
from jax.sharding import PartitionSpec as P

AXES = ("z", "core", "y", "x")
SIZES = (4, 2, 4, 4)
PEERS = 128
BLOCK = 128
PAIRS = 32
EARLY = 32
MIDDLE = 64
AHEAD = 4
MESH = pl.DeviceIdType.MESH
ANY = pl.BlockSpec(memory_space=pl.ANY)
SMEM = pl.BlockSpec(memory_space=pltpu.SMEM)
VMEM = pl.BlockSpec(memory_space=pltpu.VMEM)


def chunk(index, size):
    return pl.ds(pl.multiple_of(index * size, size), size)


def as_lanes(column):
    rows = column.shape[0]
    wide = jnp.broadcast_to(column, (rows, BLOCK))
    return jnp.transpose(wide)[0:1, :]


def routes():
    left = [offset for offset in itertools.product(*(range(size) for size in SIZES))][1:]

    def load(offset):
        links = [0] * 6
        for axis, step in enumerate((offset[0], offset[2], offset[3])):
            links[2 * axis] += step in (1, 2)
            links[2 * axis + 1] += step in (2, 3)
        return links

    used = [0] * 6
    order = []
    while left:
        def spread(offset):
            after = [a + b for a, b in zip(used, load(offset))]
            return max(after) - min(after)

        best = min(left, key=spread)
        left.remove(best)
        used = [a + b for a, b in zip(used, load(best))]
        order.append(best)
    return order


def three_terms(value):
    terms = []
    for _ in range(3):
        term = value.astype(jnp.bfloat16)
        terms.append(term)
        value = value - term.astype(jnp.float32)
    return terms


def exchange(
    index_ref, target_ref, slot_ref, target_area_ref, area_ref, source_ref, weight_ref,
    in_ref, total_ref,
    source, weights, blocks, areas, pair_rows, slot_rows, back, own, others,
    send_sem, recv_sem, near_sem, source_sem, weight_sem,
    back_send_sem, back_sem, mass_send_sem, mass_sem,
):
    here = [lax.axis_index(axis) for axis in AXES]
    turned = [[lax.rem(h + k, size) for k in range(size)] for h, size in zip(here, SIZES)]
    offsets = routes()
    opposite = [
        offsets.index(tuple((-k) % size for k, size in zip(offset, SIZES)))
        for offset in offsets
    ]

    def number(place):
        value = place[0]
        for size, part in zip(SIZES[1:], place[1:]):
            value = value * size + part
        return value

    places = [tuple(axis[k] for axis, k in zip(turned, offset)) for offset in offsets]
    me = number(here)
    last = PEERS - 1
    rows = source.shape[0]
    pairs = weights.shape[0]
    barrier = pltpu.get_barrier_semaphore()
    far = pltpu.make_async_copy(source_ref, source, source_sem)
    far.start()
    for place in places:
        pl.semaphore_signal(barrier, inc=1, device_id=place, device_id_type=MESH)
    for part in range(pairs // PAIRS):
        span = pl.ds(part * PAIRS, PAIRS)
        pltpu.make_async_copy(
            weight_ref.at[span], weights.at[span], weight_sem.at[part]
        ).start()

    def gather(k):
        peer = me if k == last else number(places[k])
        for slot in range(blocks.shape[1]):
            block = jnp.maximum(index_ref[0, slot, peer], 0)
            blocks[k, slot] = source[:, pl.ds(block * BLOCK, BLOCK)]

    def send(k):
        pltpu.make_async_remote_copy(
            src_ref=blocks.at[k],
            dst_ref=in_ref.at[me],
            send_sem=send_sem,
            recv_sem=recv_sem,
            device_id=places[k],
            device_id_type=MESH,
        ).start()

    far.wait()
    for k in range(EARLY):
        gather(k)
    pl.semaphore_wait(barrier, PEERS - 1)
    for k in range(EARLY):
        send(k)
    for k in range(EARLY, PEERS):
        gather(k)
    kept = pltpu.make_async_copy(blocks.at[last], in_ref.at[me], near_sem)
    kept.start()

    area = target_area_ref[...]
    high = area.astype(jnp.bfloat16)
    low = (area - high.astype(jnp.float32)).astype(jnp.bfloat16)
    areas[:, 0:8, :] = jnp.broadcast_to(high[:, None, :], (area.shape[0], 8, BLOCK))
    areas[:, 8:16, :] = jnp.broadcast_to(low[:, None, :], (area.shape[0], 8, BLOCK))

    def part_of(part, _):
        span = chunk(part, PAIRS)
        pltpu.make_async_copy(
            weight_ref.at[span], weights.at[span], weight_sem.at[part]
        ).wait()
        for i in range(PAIRS):
            pair = part * PAIRS + i
            product = lax.dot_general(
                areas[target_ref[pair]],
                weights[pair],
                (((1,), (1,)), ((), ())),
                preferred_element_type=jnp.float32,
            )
            row = product[0:8] + product[8:16]
            pair_rows[pl.ds(pair, 1), :] = row[0:1]
        return 0

    lax.fori_loop(0, pairs // PAIRS, part_of, 0)
    terms = three_terms(pair_rows[...])
    peer = lax.broadcasted_iota(jnp.int32, (PEERS, pairs), 0)
    capacity = blocks.shape[1]
    for slot in range(capacity):
        chosen = jnp.where(peer * capacity + slot == slot_ref[...], 1.0, 0.0)
        chosen = chosen.astype(jnp.bfloat16)
        slot_rows[:, slot, :] = sum(
            jnp.dot(chosen, term, preferred_element_type=jnp.float32) for term in terms
        )
    back[last] = slot_rows[me]
    for k in range(last):
        pltpu.make_async_remote_copy(
            src_ref=slot_rows.at[number(places[k])],
            dst_ref=back.at[opposite[k]],
            send_sem=back_send_sem,
            recv_sem=back_sem,
            device_id=places[k],
            device_id_type=MESH,
        ).start()
    for k in range(EARLY, MIDDLE):
        send(k)

    def source_part(part, total):
        columns = chunk(part, BLOCK)
        return total + source[:, columns].astype(jnp.float32) * area_ref[:, columns]

    zero = jnp.zeros((rows, BLOCK), jnp.float32)
    count = source.shape[1] // BLOCK
    source_total = lax.fori_loop(0, count, source_part, zero, unroll=8)
    most = pl.ds(0, last)
    pltpu.make_async_copy(slot_rows.at[most], back.at[most], back_sem).wait()

    def target_part(peer, total):
        for slot in range(capacity):
            factors = back[peer, pl.ds(slot, 1), :]
            total += blocks[peer, slot].astype(jnp.float32) * factors
        return total

    target_total = lax.fori_loop(0, PEERS, target_part, zero, unroll=4)
    column = jnp.concatenate(
        [
            jnp.sum(source_total, axis=1, keepdims=True),
            jnp.sum(target_total, axis=1, keepdims=True),
        ],
        axis=0,
    )
    own[...] = as_lanes(column)
    others[me] = own[...]
    for k in range(last):
        pltpu.make_async_remote_copy(
            src_ref=own,
            dst_ref=others.at[me],
            send_sem=mass_send_sem,
            recv_sem=mass_sem,
            device_id=places[k],
            device_id_type=MESH,
        ).start()
    for k in range(MIDDLE, last):
        send(k)
    pltpu.make_async_copy(others.at[most], others.at[most], mass_sem).wait()
    total = others[0]
    for k in range(1, PEERS):
        total += others[k]
    total_ref[...] = total
    pltpu.make_async_copy(others.at[most], others.at[most], mass_send_sem).wait()
    pltpu.make_async_copy(slot_rows.at[most], back.at[most], back_send_sem).wait()
    kept.wait()
    pltpu.make_async_copy(blocks.at[most], in_ref.at[most], send_sem).wait()
    pltpu.make_async_copy(blocks.at[most], in_ref.at[most], recv_sem).wait()


def exchanged(send_index, pair_slot, pair_target, target_area, area, source, weights):
    rows = source.shape[0]
    peers, capacity = send_index.shape[1:]
    targets = target_area.shape[0]
    pairs = weights.shape[0]
    blocks = (peers, capacity, rows, BLOCK)
    return pl.pallas_call(
        exchange,
        out_shape=(
            jax.ShapeDtypeStruct(blocks, source.dtype),
            jax.ShapeDtypeStruct((1, 2 * rows), jnp.float32),
        ),
        in_specs=[SMEM, SMEM, VMEM, VMEM, VMEM, ANY, ANY],
        out_specs=(ANY, VMEM),
        scratch_shapes=[
            pltpu.VMEM(source.shape, source.dtype),
            pltpu.VMEM(weights.shape, weights.dtype),
            pltpu.VMEM(blocks, source.dtype),
            pltpu.VMEM((targets, 16, BLOCK), jnp.bfloat16),
            pltpu.VMEM((pairs, BLOCK), jnp.float32),
            pltpu.VMEM((peers, capacity, BLOCK), jnp.float32),
            pltpu.VMEM((peers, capacity, BLOCK), jnp.float32),
            pltpu.VMEM((1, 2 * rows), jnp.float32),
            pltpu.VMEM((peers, 1, 2 * rows), jnp.float32),
        ]
        + [pltpu.SemaphoreType.DMA] * 4
        + [pltpu.SemaphoreType.DMA((pairs // PAIRS,))]
        + [pltpu.SemaphoreType.DMA] * 4,
        compiler_params=pltpu.CompilerParams(collective_id=1, has_side_effects=True),
    )(
        jnp.swapaxes(send_index, 1, 2),
        pair_target,
        pair_slot[None, :],
        target_area,
        area,
        source,
        weights,
    )


def regrid(
    slot_ref, target_ref, total_ref, source_ref, weight_ref, out_ref,
    source, weights, source_sem, weight_sem,
):
    parts = weights.shape[0] // PAIRS

    def fetch(part):
        span = chunk(part, PAIRS)
        return pltpu.make_async_copy(
            weight_ref.at[span], weights.at[span], weight_sem.at[part]
        )

    far = pltpu.make_async_copy(source_ref, source, source_sem)
    far.start()
    for part in range(AHEAD):
        fetch(part).start()
    out_ref[...] = jnp.zeros_like(out_ref)
    far.wait()

    def part_of(part, _):
        @pl.when(part + AHEAD < parts)
        def _():
            fetch(part + AHEAD).start()

        fetch(part).wait()
        for i in range(PAIRS):
            pair = part * PAIRS + i
            product = jnp.dot(
                source[slot_ref[pair]], weights[pair], preferred_element_type=jnp.float32
            )
            out_ref[:, chunk(target_ref[pair], BLOCK)] += product
        return 0

    lax.fori_loop(0, parts, part_of, 0)
    rows, cells = out_ref.shape
    total = jnp.transpose(jnp.broadcast_to(total_ref[...], (BLOCK, BLOCK)))
    scale = total[:rows] / total[rows : 2 * rows]
    for t in range(cells // BLOCK):
        columns = pl.ds(t * BLOCK, BLOCK)
        out_ref[:, columns] = out_ref[:, columns] * scale


def target_blocks(pair_slot, pair_target, inbound, weights, total, cells):
    slots, rows, _ = inbound.shape
    pairs = weights.shape[0]
    return pl.pallas_call(
        regrid,
        out_shape=jax.ShapeDtypeStruct((rows, cells), jnp.float32),
        in_specs=[SMEM, SMEM, VMEM, ANY, ANY],
        out_specs=VMEM,
        scratch_shapes=[
            pltpu.VMEM(inbound.shape, inbound.dtype),
            pltpu.VMEM(weights.shape, weights.dtype),
            pltpu.SemaphoreType.DMA,
            pltpu.SemaphoreType.DMA((pairs // PAIRS,)),
        ],
    )(pair_slot, pair_target, total, inbound, weights)


def shards(src_field, src_area, tgt_area, weights, send_index, pair_slot, pair_target):
    rows = src_field.shape[0]
    peers, capacity = send_index.shape[1:]
    inbound, total = exchanged(
        send_index,
        pair_slot,
        pair_target,
        tgt_area.reshape(-1, BLOCK),
        src_area[None, :],
        src_field,
        weights,
    )
    inbound = inbound.reshape(peers * capacity, rows, BLOCK)
    return target_blocks(
        pair_slot, pair_target, inbound, weights, total, tgt_area.shape[0]
    )


def solution(mesh):
    split = Mesh(mesh.devices.reshape(SIZES), AXES)
    placed = (
        P(None, AXES),
        P(AXES),
        P(AXES),
        P(AXES, None, None),
        P(AXES, None, None),
        P(AXES),
        P(AXES),
    )
    return jax.shard_map(
        shards, mesh=split, in_specs=placed, out_specs=P(None, AXES), check_vma=False
    )
```

time: 95.1 us -> 75.7 us (0.80)
  Pallas kernels: 94.1 us -> 73.3 us
  local copies, waits for them, and re-layouts: 0 us -> 1.24 us
    pallas_call x2 -> x1, Pallas kernels: 80.8 us -> 62.3 us  [exchanged(): pl.pallas_call(exchange, out_shape=(jax.ShapeDtypeStruct(blocks, source.d...]
    pallas_call x1, Pallas kernels: 13.3 us -> 10.9 us  [target_blocks(): pl.pallas_call(regrid, out_shape=jax.ShapeDtypeStruct((rows, cells), jnp....]
    broadcast_in_dim x0 -> x1, local copies, waits for them, and re-layouts: none -> 1.24 us  [exchanged(): pair_slot[None, :]]
where the time goes in v4:
time: 75.7 us; the launch traced here: 74.5 us
  Pallas kernels  73.3 us (97%)
  local copies, waits for them, and re-layouts  1.24 us (2%)
    pallas_call x1, Pallas kernels, exchanged(): pl.pallas_call(exchange, out_shape=(jax.ShapeDtypeStruct(blocks, source.d...  62.3 us
    pallas_call x1, Pallas kernels, target_blocks(): pl.pallas_call(regrid, out_shape=jax.ShapeDtypeStruct((rows, cells), jnp....  10.9 us

profile of v4, /device:TPU:0, one launch (start us, length us, event | category | flops | bytes accessed | tf_op | source)
XLA Modules:
  0.0 74.5 jit_solution(606197379949428211)
XLA Ops:
  0.0 1.2 %broadcast_in_dim.6.slot_ref = s32[1,384]{1,0:T(1,128)} reshape(s32[384]{0:T(512)} %slot_ref.1) | data formatting | bytes 3072 | tf_op jit(solution)/shard_map/broadcast_in_dim | solution.py:259
  1.2 62.3 %shard_map.73 = (bf16[128,2,64,128]{3,2,1,0:T(8,128)(2,1)}, f32[1,128]{1,0:T(1,128)}) custom-call(s32[1,2,128]{2,1,0:T(2,128)} %bitcast.7, s32[384]{0:T(512)} %target_ref.3, s32[1,384]{1,0:T(1,128)} %broadcast_in_dim.6.slot_ref, f32[64,128]{1,0:T(8,128)} %bitcast.6, f32[1,32768]{1,0:T(1,128)} %bitcast.5, bf16[64,32768]{1,0:T(8,128)(2,1)} %source_ref.1, ...), custom_call_target="tpu_custom_call" | custom-call | tf_op jit(solution)/shard_map/pallas_call | solution.py:233
  63.6 10.9 %shard_map.74 = f32[64,8192]{1,0:T(8,128)} custom-call(s32[384]{0:T(512)} %slot_ref.1, s32[384]{0:T(512)} %target_ref.3, f32[1,128]{1,0:T(1,128)} %get-tuple-element.7.total_ref, bf16[256,64,128]{2,1,0:T(8,128)(2,1)} %bitcast.4, bf16[384,128,128]{2,1,0:T(8,128)(2,1)} %weight_ref.3), custom_call_target="tpu_custom_call" | custom-call | tf_op jit(solution)/shard_map/pallas_call | solution.py:312

commit v5 on v4

--- a/solution.py
+++ b/solution.py
@@ -15,9 +15,11 @@
 PAIRS = 32
 EARLY = 32
 MIDDLE = 64
-AHEAD = 4
+EXCHANGE_VMEM = 36 * 1024 * 1024
+REGRID_VMEM = 24 * 1024 * 1024
 MESH = pl.DeviceIdType.MESH
 ANY = pl.BlockSpec(memory_space=pl.ANY)
+HBM = pl.BlockSpec(memory_space=pltpu.HBM)
 SMEM = pl.BlockSpec(memory_space=pltpu.SMEM)
 VMEM = pl.BlockSpec(memory_space=pltpu.VMEM)
 
@@ -66,10 +68,11 @@
 
 
 def exchange(
-    index_ref, target_ref, slot_ref, target_area_ref, area_ref, source_ref, weight_ref,
-    in_ref, total_ref,
-    source, weights, blocks, areas, pair_rows, slot_rows, back, own, others,
-    send_sem, recv_sem, near_sem, source_sem, weight_sem,
+    index_hbm, target_hbm, slot_hbm, target_area_hbm, area_hbm, source_ref, weight_ref,
+    in_ref, total_ref, weights,
+    index_ref, target_ref, slot_ref, target_area_ref, area_ref,
+    source, blocks, areas, pair_rows, slot_rows, back, own, others,
+    send_sem, recv_sem, source_sem, weight_sem, small_sem,
     back_send_sem, back_sem, mass_send_sem, mass_sem,
 ):
     here = [lax.axis_index(axis) for axis in AXES]
@@ -94,14 +97,22 @@
     barrier = pltpu.get_barrier_semaphore()
     far = pltpu.make_async_copy(source_ref, source, source_sem)
     far.start()
+    small = [
+        pltpu.make_async_copy(whole, held, small_sem.at[i])
+        for i, (whole, held) in enumerate(
+            (
+                (index_hbm, index_ref),
+                (target_hbm, target_ref),
+                (slot_hbm, slot_ref),
+                (target_area_hbm, target_area_ref),
+                (area_hbm, area_ref),
+            )
+        )
+    ]
+    for copy in small:
+        copy.start()
     for place in places:
         pl.semaphore_signal(barrier, inc=1, device_id=place, device_id_type=MESH)
-    for part in range(pairs // PAIRS):
-        span = pl.ds(part * PAIRS, PAIRS)
-        pltpu.make_async_copy(
-            weight_ref.at[span], weights.at[span], weight_sem.at[part]
-        ).start()
-
     def gather(k):
         peer = me if k == last else number(places[k])
         for slot in range(blocks.shape[1]):
@@ -118,7 +129,14 @@
             device_id_type=MESH,
         ).start()
 
+    for copy in small:
+        copy.wait()
     far.wait()
+    for part in range(pairs // PAIRS):
+        span = pl.ds(part * PAIRS, PAIRS)
+        pltpu.make_async_copy(
+            weight_ref.at[span], weights.at[span], weight_sem.at[part]
+        ).start()
     for k in range(EARLY):
         gather(k)
     pl.semaphore_wait(barrier, PEERS - 1)
@@ -126,8 +144,7 @@
         send(k)
     for k in range(EARLY, PEERS):
         gather(k)
-    kept = pltpu.make_async_copy(blocks.at[last], in_ref.at[me], near_sem)
-    kept.start()
+    in_ref[me] = blocks[last]
 
     area = target_area_ref[...]
     high = area.astype(jnp.bfloat16)
@@ -154,14 +171,20 @@
 
     lax.fori_loop(0, pairs // PAIRS, part_of, 0)
     terms = three_terms(pair_rows[...])
-    peer = lax.broadcasted_iota(jnp.int32, (PEERS, pairs), 0)
+    peer = lax.broadcasted_iota(jnp.int32, (PEERS, BLOCK), 0)
     capacity = blocks.shape[1]
     for slot in range(capacity):
-        chosen = jnp.where(peer * capacity + slot == slot_ref[...], 1.0, 0.0)
-        chosen = chosen.astype(jnp.bfloat16)
-        slot_rows[:, slot, :] = sum(
-            jnp.dot(chosen, term, preferred_element_type=jnp.float32) for term in terms
-        )
+        rows_of = jnp.zeros((PEERS, BLOCK), jnp.float32)
+        for part in range(pairs // BLOCK):
+            span = slice(part * BLOCK, (part + 1) * BLOCK)
+            named = slot_ref[part : part + 1, :]
+            chosen = jnp.where(peer * capacity + slot == named, 1.0, 0.0)
+            chosen = chosen.astype(jnp.bfloat16)
+            for term in terms:
+                rows_of += jnp.dot(
+                    chosen, term[span], preferred_element_type=jnp.float32
+                )
+        slot_rows[:, slot, :] = rows_of
     back[last] = slot_rows[me]
     for k in range(last):
         pltpu.make_async_remote_copy(
@@ -219,7 +242,6 @@
     total_ref[...] = total
     pltpu.make_async_copy(others.at[most], others.at[most], mass_send_sem).wait()
     pltpu.make_async_copy(slot_rows.at[most], back.at[most], back_send_sem).wait()
-    kept.wait()
     pltpu.make_async_copy(blocks.at[most], in_ref.at[most], send_sem).wait()
     pltpu.make_async_copy(blocks.at[most], in_ref.at[most], recv_sem).wait()
 
@@ -233,14 +255,19 @@
     return pl.pallas_call(
         exchange,
         out_shape=(
-            jax.ShapeDtypeStruct(blocks, source.dtype),
+            pltpu.VMEM(blocks, source.dtype),
             jax.ShapeDtypeStruct((1, 2 * rows), jnp.float32),
+            pltpu.VMEM(weights.shape, weights.dtype),
         ),
-        in_specs=[SMEM, SMEM, VMEM, VMEM, VMEM, ANY, ANY],
-        out_specs=(ANY, VMEM),
+        in_specs=[HBM] * 7,
+        out_specs=(VMEM, VMEM, VMEM),
         scratch_shapes=[
+            pltpu.SMEM((1, capacity, peers), jnp.int32),
+            pltpu.SMEM((pairs,), jnp.int32),
+            pltpu.VMEM((pairs // BLOCK, BLOCK), jnp.int32),
+            pltpu.VMEM(target_area.shape, jnp.float32),
+            pltpu.VMEM(area.shape, jnp.float32),
             pltpu.VMEM(source.shape, source.dtype),
-            pltpu.VMEM(weights.shape, weights.dtype),
             pltpu.VMEM(blocks, source.dtype),
             pltpu.VMEM((targets, 16, BLOCK), jnp.bfloat16),
             pltpu.VMEM((pairs, BLOCK), jnp.float32),
@@ -249,50 +276,39 @@
             pltpu.VMEM((1, 2 * rows), jnp.float32),
             pltpu.VMEM((peers, 1, 2 * rows), jnp.float32),
         ]
-        + [pltpu.SemaphoreType.DMA] * 4
-        + [pltpu.SemaphoreType.DMA((pairs // PAIRS,))]
+        + [pltpu.SemaphoreType.DMA] * 3
+        + [pltpu.SemaphoreType.DMA((pairs // PAIRS,)), pltpu.SemaphoreType.DMA((5,))]
         + [pltpu.SemaphoreType.DMA] * 4,
-        compiler_params=pltpu.CompilerParams(collective_id=1, has_side_effects=True),
+        compiler_params=pltpu.CompilerParams(
+            collective_id=1, has_side_effects=True, vmem_limit_bytes=EXCHANGE_VMEM
+        ),
     )(
-        jnp.swapaxes(send_index, 1, 2),
-        pair_target,
-        pair_slot[None, :],
-        target_area,
-        area,
-        source,
-        weights,
-    )
-
-
-def regrid(
-    slot_ref, target_ref, total_ref, source_ref, weight_ref, out_ref,
-    source, weights, source_sem, weight_sem,
-):
-    parts = weights.shape[0] // PAIRS
-
-    def fetch(part):
-        span = chunk(part, PAIRS)
-        return pltpu.make_async_copy(
-            weight_ref.at[span], weights.at[span], weight_sem.at[part]
+        *(
+            pltpu.with_memory_space_constraint(operand, pltpu.HBM)
+            for operand in (
+                jnp.swapaxes(send_index, 1, 2),
+                pair_target,
+                pair_slot.reshape(-1, BLOCK),
+                target_area,
+                area,
+                source,
+                weights,
+            )
         )
-
-    far = pltpu.make_async_copy(source_ref, source, source_sem)
-    far.start()
-    for part in range(AHEAD):
-        fetch(part).start()
+    )
+
+
+def regrid(slot_ref, target_ref, total_ref, source_ref, weight_ref, out_ref):
+    parts = weight_ref.shape[0] // PAIRS
     out_ref[...] = jnp.zeros_like(out_ref)
-    far.wait()
 
     def part_of(part, _):
-        @pl.when(part + AHEAD < parts)
-        def _():
-            fetch(part + AHEAD).start()
-
-        fetch(part).wait()
         for i in range(PAIRS):
             pair = part * PAIRS + i
             product = jnp.dot(
-                source[slot_ref[pair]], weights[pair], preferred_element_type=jnp.float32
+                source_ref[slot_ref[pair]],
+                weight_ref[pair],
+                preferred_element_type=jnp.float32,
             )
             out_ref[:, chunk(target_ref[pair], BLOCK)] += product
         return 0
@@ -307,26 +323,20 @@
 
 
 def target_blocks(pair_slot, pair_target, inbound, weights, total, cells):
-    slots, rows, _ = inbound.shape
-    pairs = weights.shape[0]
+    rows = inbound.shape[1]
     return pl.pallas_call(
         regrid,
         out_shape=jax.ShapeDtypeStruct((rows, cells), jnp.float32),
-        in_specs=[SMEM, SMEM, VMEM, ANY, ANY],
+        in_specs=[SMEM, SMEM, VMEM, VMEM, VMEM],
         out_specs=VMEM,
-        scratch_shapes=[
-            pltpu.VMEM(inbound.shape, inbound.dtype),
-            pltpu.VMEM(weights.shape, weights.dtype),
-            pltpu.SemaphoreType.DMA,
-            pltpu.SemaphoreType.DMA((pairs // PAIRS,)),
-        ],
+        compiler_params=pltpu.CompilerParams(vmem_limit_bytes=REGRID_VMEM),
     )(pair_slot, pair_target, total, inbound, weights)
 
 
 def shards(src_field, src_area, tgt_area, weights, send_index, pair_slot, pair_target):
     rows = src_field.shape[0]
     peers, capacity = send_index.shape[1:]
-    inbound, total = exchanged(
+    inbound, total, held = exchanged(
         send_index,
         pair_slot,
         pair_target,
@@ -337,7 +347,7 @@
     )
     inbound = inbound.reshape(peers * capacity, rows, BLOCK)
     return target_blocks(
-        pair_slot, pair_target, inbound, weights, total, tgt_area.shape[0]
+        pair_slot, pair_target, inbound, held, total, tgt_area.shape[0]
     )
 
 

time: 75.7 us -> 69.6 us (0.919)
  Pallas kernels: 73.3 us -> 68.4 us
  local copies, waits for them, and re-layouts: 1.24 us -> 0.01 us
    pallas_call x1, Pallas kernels: 10.9 us -> 7.58 us  [target_blocks(): pl.pallas_call(regrid, out_shape=jax.ShapeDtypeStruct((rows, cells), jnp....]
    pallas_call x1, Pallas kernels: 62.3 us -> 60.9 us  [exchanged(): pl.pallas_call(exchange, out_shape=(pltpu.VMEM(blocks, source.dtype), jax...]
    broadcast_in_dim x1 -> x0, local copies, waits for them, and re-layouts: 1.24 us -> none  [exchanged(): pair_slot[None, :]]
where the time goes in v5:
time: 69.6 us; the launch traced here: 68.5 us
  Pallas kernels  68.4 us (98%)
    pallas_call x1, Pallas kernels, exchanged(): pl.pallas_call(exchange, out_shape=(pltpu.VMEM(blocks, source.dtype), jax...  60.9 us
    pallas_call x1, Pallas kernels, target_blocks(): pl.pallas_call(regrid, out_shape=jax.ShapeDtypeStruct((rows, cells), jnp....  7.58 us

profile of v5, /device:TPU:0, one launch (start us, length us, event | category | flops | bytes accessed | tf_op | source)
XLA Modules:
  0.0 68.5 jit_solution(919470693775133622)
XLA Ops:
  0.0 0.0 copy-start
  0.0 0.0 copy-start.1
  0.0 60.9 %shard_map.73 = (bf16[128,2,64,128]{3,2,1,0:T(8,128)(2,1)S(1)}, f32[1,128]{1,0:T(1,128)S(1)}, bf16[384,128,128]{2,1,0:T(8,128)(2,1)S(1)}) custom-call(s32[1,2,128]{2,1,0:T(2,128)} %bitcast.9, s32[384]{0:T(512)} %target_ref.1, s32[3,128]{1,0:T(4,128)} %bitcast.6, f32[64,128]{1,0:T(8,128)} %bitcast.8, f32[1,32768]{1,0:T(1,128)} %bitcast.7, ...), custom_call_target="tpu_custom_call" | custom-call | tf_op jit(solution)/shard_map/pallas_call | solution.py:255
  60.9 0.0 copy-done
  60.9 0.0 copy-done.1
  60.9 7.6 %shard_map.74 = f32[64,8192]{1,0:T(8,128)} custom-call(s32[384]{0:T(512)S(1)} %copy-done, s32[384]{0:T(512)S(1)} %copy-done.1, f32[1,128]{1,0:T(1,128)S(1)} %get-tuple-element.8.total_ref, bf16[256,64,128]{2,1,0:T(8,128)(2,1)S(1)} %bitcast.5, bf16[384,128,128]{2,1,0:T(8,128)(2,1)S(1)} %get-tuple-element.10.weight_ref), custom_call_target="tpu_custom_call" | custom-call | tf_op jit(solution)/shard_map/pallas_call | solution.py:327
Async XLA Ops:
  0.0 60.9 %copy-start = (s32[384]{0:T(512)S(1)}, s32[384]{0:T(512)}, u32[]{:S(2)}) copy-start(s32[384]{0:T(512)} %slot_ref.1) | copy-start | bytes 4612
  0.0 60.9 %copy-start.1 = (s32[384]{0:T(512)S(1)}, s32[384]{0:T(512)}, u32[]{:S(2)}) copy-start(s32[384]{0:T(512)} %target_ref.1) | copy-start | bytes 4612

commit v6 on v5

--- a/solution.py
+++ b/solution.py
@@ -13,6 +13,7 @@
 PEERS = 128
 BLOCK = 128
 PAIRS = 32
+PIECES = 4
 EARLY = 32
 MIDDLE = 64
 EXCHANGE_VMEM = 36 * 1024 * 1024
@@ -298,9 +299,23 @@
     )
 
 
-def regrid(slot_ref, target_ref, total_ref, source_ref, weight_ref, out_ref):
+def regrid(
+    slot_hbm, target_hbm, total_ref, source_ref, weight_ref, out_hbm,
+    slot_ref, target_ref, out_ref, small_sem, out_sem,
+):
     parts = weight_ref.shape[0] // PAIRS
+    small = [
+        pltpu.make_async_copy(slot_hbm, slot_ref, small_sem.at[0]),
+        pltpu.make_async_copy(target_hbm, target_ref, small_sem.at[1]),
+    ]
+    for copy in small:
+        copy.start()
+    rows, cells = out_ref.shape
+    total = jnp.transpose(jnp.broadcast_to(total_ref[...], (BLOCK, BLOCK)))
+    scale = total[:rows] / total[rows : 2 * rows]
     out_ref[...] = jnp.zeros_like(out_ref)
+    for copy in small:
+        copy.wait()
 
     def part_of(part, _):
         for i in range(PAIRS):
@@ -314,12 +329,23 @@
         return 0
 
     lax.fori_loop(0, parts, part_of, 0)
-    rows, cells = out_ref.shape
-    total = jnp.transpose(jnp.broadcast_to(total_ref[...], (BLOCK, BLOCK)))
-    scale = total[:rows] / total[rows : 2 * rows]
-    for t in range(cells // BLOCK):
-        columns = pl.ds(t * BLOCK, BLOCK)
-        out_ref[:, columns] = out_ref[:, columns] * scale
+    width = cells // PIECES
+
+    def leave(piece):
+        columns = pl.ds(piece * width, width)
+        return pltpu.make_async_copy(
+            out_ref.at[:, columns], out_hbm.at[:, columns], out_sem.at[piece]
+        )
+
+    for piece in range(PIECES):
+        for t in range(width // BLOCK):
+            columns = pl.ds(piece * width + t * BLOCK, BLOCK)
+            out_ref[:, columns] = out_ref[:, columns] * scale
+        if piece > 0:
+            leave(piece - 1).start()
+    leave(PIECES - 1).start()
+    for piece in range(PIECES):
+        leave(piece).wait()
 
 
 def target_blocks(pair_slot, pair_target, inbound, weights, total, cells):
@@ -327,10 +353,23 @@
     return pl.pallas_call(
         regrid,
         out_shape=jax.ShapeDtypeStruct((rows, cells), jnp.float32),
-        in_specs=[SMEM, SMEM, VMEM, VMEM, VMEM],
-        out_specs=VMEM,
+        in_specs=[HBM, HBM, VMEM, VMEM, VMEM],
+        out_specs=ANY,
+        scratch_shapes=[
+            pltpu.SMEM(pair_slot.shape, jnp.int32),
+            pltpu.SMEM(pair_target.shape, jnp.int32),
+            pltpu.VMEM((rows, cells), jnp.float32),
+            pltpu.SemaphoreType.DMA((2,)),
+            pltpu.SemaphoreType.DMA((PIECES,)),
+        ],
         compiler_params=pltpu.CompilerParams(vmem_limit_bytes=REGRID_VMEM),
-    )(pair_slot, pair_target, total, inbound, weights)
+    )(
+        pltpu.with_memory_space_constraint(pair_slot, pltpu.HBM),
+        pltpu.with_memory_space_constraint(pair_target, pltpu.HBM),
+        total,
+        inbound,
+        weights,
+    )
 
 
 def shards(src_field, src_area, tgt_area, weights, send_index, pair_slot, pair_target):

time: 69.6 us -> 69.5 us (level)
  no operation moved by 1% of the time
where the time goes in v6:
time: 69.5 us; the launch traced here: 68.3 us
  Pallas kernels  68.3 us (98%)
    pallas_call x1, Pallas kernels, exchanged(): pl.pallas_call(exchange, out_shape=(pltpu.VMEM(blocks, source.dtype), jax...  60.7 us
    pallas_call x1, Pallas kernels, target_blocks(): pl.pallas_call(regrid, out_shape=jax.ShapeDtypeStruct((rows, cells), jnp....  7.59 us

profile of v6, /device:TPU:0, one launch (start us, length us, event | category | flops | bytes accessed | tf_op | source)
XLA Modules:
  0.0 68.3 jit_solution(18445025443840453045)
XLA Ops:
  0.0 60.7 %shard_map.73 = (bf16[128,2,64,128]{3,2,1,0:T(8,128)(2,1)S(1)}, f32[1,128]{1,0:T(1,128)S(1)}, bf16[384,128,128]{2,1,0:T(8,128)(2,1)S(1)}) custom-call(s32[1,2,128]{2,1,0:T(2,128)} %bitcast.9, s32[384]{0:T(512)} %target_hbm.3, s32[3,128]{1,0:T(4,128)} %bitcast.8, f32[64,128]{1,0:T(8,128)} %bitcast.7, f32[1,32768]{1,0:T(1,128)} %bitcast.6, ...), custom_call_target="tpu_custom_call" | custom-call | tf_op jit(solution)/shard_map/pallas_call | solution.py:256
  60.8 7.6 %shard_map.74 = f32[64,8192]{1,0:T(8,128)} custom-call(s32[384]{0:T(512)} %slot_hbm.1, s32[384]{0:T(512)} %target_hbm.3, f32[1,128]{1,0:T(1,128)S(1)} %get-tuple-element.8.total_ref, bf16[256,64,128]{2,1,0:T(8,128)(2,1)S(1)} %bitcast.5, bf16[384,128,128]{2,1,0:T(8,128)(2,1)S(1)} %get-tuple-element.10.weight_ref), custom_call_target="tpu_custom_call" | custom-call | tf_op jit(solution)/shard_map/pallas_call | solution.py:353

commit v7 on v6

--- a/solution.py
+++ b/solution.py
@@ -14,8 +14,8 @@
 BLOCK = 128
 PAIRS = 32
 PIECES = 4
-EARLY = 32
-MIDDLE = 64
+EARLY = 48
+MIDDLE = 96
 EXCHANGE_VMEM = 36 * 1024 * 1024
 REGRID_VMEM = 24 * 1024 * 1024
 MESH = pl.DeviceIdType.MESH

time: 69.5 us -> 69.5 us (level)
  no operation moved by 1% of the time
where the time goes in v7:
time: 69.5 us; the launch traced here: 68.1 us
  Pallas kernels  68.1 us (98%)
    pallas_call x1, Pallas kernels, exchanged(): pl.pallas_call(exchange, out_shape=(pltpu.VMEM(blocks, source.dtype), jax...  60.5 us
    pallas_call x1, Pallas kernels, target_blocks(): pl.pallas_call(regrid, out_shape=jax.ShapeDtypeStruct((rows, cells), jnp....  7.59 us

profile of v7, /device:TPU:0, one launch (start us, length us, event | category | flops | bytes accessed | tf_op | source)
XLA Modules:
  0.0 68.1 jit_solution(292789277363756267)
XLA Ops:
  0.0 60.5 %shard_map.73 = (bf16[128,2,64,128]{3,2,1,0:T(8,128)(2,1)S(1)}, f32[1,128]{1,0:T(1,128)S(1)}, bf16[384,128,128]{2,1,0:T(8,128)(2,1)S(1)}) custom-call(s32[1,2,128]{2,1,0:T(2,128)} %bitcast.9, s32[384]{0:T(512)} %target_hbm.3, s32[3,128]{1,0:T(4,128)} %bitcast.8, f32[64,128]{1,0:T(8,128)} %bitcast.7, f32[1,32768]{1,0:T(1,128)} %bitcast.6, ...), custom_call_target="tpu_custom_call" | custom-call | tf_op jit(solution)/shard_map/pallas_call | solution.py:256
  60.5 7.6 %shard_map.74 = f32[64,8192]{1,0:T(8,128)} custom-call(s32[384]{0:T(512)} %slot_hbm.1, s32[384]{0:T(512)} %target_hbm.3, f32[1,128]{1,0:T(1,128)S(1)} %get-tuple-element.8.total_ref, bf16[256,64,128]{2,1,0:T(8,128)(2,1)S(1)} %bitcast.5, bf16[384,128,128]{2,1,0:T(8,128)(2,1)S(1)} %get-tuple-element.10.weight_ref), custom_call_target="tpu_custom_call" | custom-call | tf_op jit(solution)/shard_map/pallas_call | solution.py:353
